TPU v7x, 256 devices: a whole 4x4x8 slice. The times are simulated.
256 devices in a mesh: doc: 16 (over y_lo, z), seq: 16 (over x, y_hi, core).
Axes of the slice: x: 4, y: 4 (y_hi: 2, y_lo: 2; y = y_hi * 2 + y_lo), z: 8, core: 2. Of those that a mesh axis runs over, the one named last changes fastest.
Arguments:
- queries: bfloat16 [131072, 512], P(('doc', 'seq')), parts along dimension 0, may hold values from -5 to 5
- teacher_keys: bfloat16 [131072, 128], P(('doc', 'seq')), parts along dimension 0, may hold values from -5 to 5
- teacher_values: bfloat16 [131072, 128], P(('doc', 'seq')), parts along dimension 0, may hold values from -5 to 5
- beacon_starts: int32 [8192], P(('doc', 'seq')), parts along dimension 0, may hold values from 0 to 511, as said below
Outputs:
- output_gap: bfloat16 [131072, 512], P(('doc', 'seq')), parts along dimension 0
- beacon_key_grad: float32 [8192, 128], P(('doc', 'seq')), parts along dimension 0
- beacon_value_grad: float32 [8192, 128], P(('doc', 'seq')), parts along dimension 0
There are 16 independent parts, one for each index of `doc`. A program takes and returns all parts, laid end to end along the dimension named above; each array names one. Nothing has to cross between parts.
Inputs may be any that keep to these rules, and one draw needn't show every extreme that they name: `beacon_starts`: each aligned block of 32 entries belongs to one shard of 512 tokens: its first entry is 0 and its entries rise strictly.
All inputs are finite; a program needn't handle non-finite values.
Results may differ from a plain program's by a relative error of at most 0.009.
Values may be sent and summed in bfloat16 or wider, within the bound.
No kernel may reach another device: no remote copies, remote signals or barrier semaphores. Data moves between devices by JAX's collectives and lax.ppermute only.
A program may use at most 192 MiB of HBM per device.

v0:
```python
import functools

import jax
import jax.numpy as jnp
from jax import lax
from jax.experimental import pallas as pl
from jax.experimental.pallas import tpu as pltpu
from jax.sharding import PartitionSpec as P


HEADS = 4
HEAD = 128
TOK = 512
BEAC = 32
SEQ = 16
ROWS = TOK + BEAC
SCALE = HEAD**-0.5
LOG2E = 1.4426950408889634
C2 = SCALE * LOG2E
F32 = jnp.float32
BF16 = jnp.bfloat16


def dot(a, b):
    return jnp.dot(a, b, preferred_element_type=F32)


def split_index(s):
    return s // 4, (s // 2) % 2, s % 2


def placed(s, dx, dy, dc):
    x, y, c = split_index(s)
    return ((x + dx) % 4) * 4 + (y + dy) % 2 * 2 + (c + dc) % 2


def whole(*shape):
    return pl.BlockSpec(shape, lambda: tuple(0 for _ in shape))


def prep_kernel(starts_ref, keys_ref, values_ref, packed_ref):
    packed_ref[0:TOK, 0:HEAD] = keys_ref[...]
    packed_ref[0:TOK, HEAD:] = values_ref[...]
    pos = lax.broadcasted_iota(jnp.int32, (1, TOK), 1)
    owner = jnp.full((1, TOK), -1, jnp.int32)
    for j in range(BEAC):
        owner = owner + (pos >= starts_ref[j]).astype(jnp.int32)
    rows = lax.broadcasted_iota(jnp.int32, (BEAC, TOK), 0)
    member = (rows == owner).astype(F32)
    counts = jnp.sum(member, axis=1, keepdims=True)
    member = member.astype(BF16)
    packed_ref[TOK:, 0:HEAD] = (dot(member, keys_ref[...]) / counts).astype(BF16)
    packed_ref[TOK:, HEAD:] = (dot(member, values_ref[...]) / counts).astype(BF16)


def prep(starts, keys, values):
    return pl.pallas_call(
        prep_kernel,
        out_shape=pltpu.VMEM((ROWS, 2 * HEAD), BF16),
        in_specs=[
            pl.BlockSpec(memory_space=pltpu.SMEM),
            whole(TOK, HEAD),
            whole(TOK, HEAD),
        ],
        out_specs=whole(ROWS, 2 * HEAD),
        name="prep",
    )(starts, keys, values)


WIDTH = 1024
GROUPS = HEADS * TOK // WIDTH
AUG = HEAD + 16
SUM = HEAD
TOP = HEAD + 8
PARAMS = pltpu.CompilerParams(vmem_limit_bytes=16 * 2**20)
STATE = jax.ShapeDtypeStruct((GROUPS, AUG, WIDTH), F32)
STATE_SPEC = whole(GROUPS, AUG, WIDTH)
QT_SHAPE = jax.ShapeDtypeStruct((GROUPS, HEAD, WIDTH), BF16)
QT_SPEC = whole(GROUPS, HEAD, WIDTH)
PART = 256


def span(i, width=PART):
    return slice(i * width, (i + 1) * width)


def located(h, part=None):
    if part is None:
        g, at = divmod(h * TOK, WIDTH)
        return g, slice(at, at + TOK)
    g, at = divmod(h * TOK + part * PART, WIDTH)
    return g, slice(at, at + PART)


def local_kernel(queries_ref, keys_ref, values_ref, qt_ref, state_ref, vt_sc):
    vt_sc[0:HEAD, :] = values_ref[...].T
    vt_sc[HEAD:, :] = jnp.ones((AUG - HEAD, TOK), BF16)
    causal = lax.broadcasted_iota(jnp.int32, (PART, PART), 0) <= lax.broadcasted_iota(
        jnp.int32, (PART, PART), 1
    )
    for h in range(HEADS):
        for part in range(TOK // PART):
            g, at = located(h, part)
            qt = queries_ref[span(part), span(h, HEAD)].T
            qt_ref[g, :, at] = qt
            s = dot(keys_ref[span(part), :], qt)
            s = jnp.where(causal, s, -1e30)
            top = jnp.max(s, axis=0, keepdims=True)
            if part:
                past = dot(keys_ref[0 : part * PART, :], qt)
                top = jnp.maximum(top, jnp.max(past, axis=0, keepdims=True))
            top = top * C2
            p = jnp.exp2(s * C2 - top).astype(BF16)
            acc = dot(vt_sc[:, span(part)], p)
            if part:
                p = jnp.exp2(past * C2 - top).astype(BF16)
                acc = acc + dot(vt_sc[:, 0 : part * PART], p)
            state_ref[g, 0:TOP, at] = acc[0:TOP]
            state_ref[g, TOP:, at] = jnp.broadcast_to(top, (AUG - TOP, PART))


def cost(blocks):
    n = HEADS * TOK * TOK * blocks
    return pl.CostEstimate(flops=n * 4 * HEAD, transcendentals=n, bytes_accessed=2**20)


def local(queries, keys, values):
    return pl.pallas_call(
        local_kernel,
        out_shape=(QT_SHAPE, STATE),
        in_specs=[whole(TOK, HEADS * HEAD), whole(TOK, HEAD), whole(TOK, HEAD)],
        out_specs=(QT_SPEC, STATE_SPEC),
        scratch_shapes=[pltpu.VMEM((AUG, TOK), BF16)],
        cost_estimate=cost(1),
        compiler_params=PARAMS,
        name="local",
    )(*[pltpu.with_memory_space_constraint(a, pltpu.HBM) for a in (queries, keys, values)])


def blocks_kernel(sides, start, fresh, pooled, places, me_ref, *refs):
    count = len(places)
    groups = len(sides) * GROUPS
    me = me_ref[0]
    qt_refs, refs = refs[: len(sides)], refs[len(sides) :]
    in_ref, refs = refs[0], refs[1:]
    block_refs, refs = refs[:count], refs[count:]
    acc_ref, refs = refs[0], refs[1:]
    if pooled:
        beacons_ref, refs = refs[0], refs[1:]
    qt_sc, m_sc, k_sc, vt_sc, s_sc, p_sc, top_sc, alpha_sc, tile_ref = refs
    for g in range(groups):
        qt_sc[g] = qt_refs[g // GROUPS][g % GROUPS]
        if g < groups - fresh:
            acc_ref[g] = in_ref[start + g]
            m_sc[g] = in_ref[start + g, TOP : TOP + 1, :]
        else:
            acc_ref[g] = jnp.zeros((AUG, WIDTH), F32)
            m_sc[g] = jnp.full((1, WIDTH), -1e30, F32)
    tiles = jnp.int32(0)
    for i in range(count):
        k_sc[i] = block_refs[i][0:TOK, 0:HEAD]
        vt_sc[i, 0:HEAD, :] = block_refs[i][0:TOK, HEAD:].T
        vt_sc[i, HEAD:, :] = jnp.ones((AUG - HEAD, TOK), BF16)
        if pooled:
            beacons_ref[i] = block_refs[i][TOK:, :]
        for n, side in enumerate(sides):
            seen = (placed(me, *places[i]) < placed(me, 0, 0, side)).astype(jnp.int32)
            for g in range(GROUPS):
                tile_ref[tiles] = i * groups + n * GROUPS + g
                tiles = tiles + seen

    def where_is(t):
        tile = tile_ref[t]
        return tile // groups, tile % groups

    def score(t):
        i, g = where_is(t)
        s = dot(k_sc[i], qt_sc[g])
        s_sc[...] = s
        top_sc[...] = jnp.max(s, axis=0, keepdims=True) * C2

    def weigh(t):
        _, g = where_is(t)
        old = m_sc[g]
        top = jnp.maximum(old, top_sc[...])
        m_sc[g] = top
        alpha_sc[...] = jnp.exp2(old - top)
        p_sc[...] = jnp.exp2(s_sc[...] * C2 - top).astype(BF16)

    def gather(t):
        i, g = where_is(t)
        acc_ref[g] = acc_ref[g] * alpha_sc[...] + dot(vt_sc[i], p_sc[...])

    def step(t, carry):
        gather(jnp.maximum(t - 1, 0))
        weigh(t)
        score(jnp.minimum(t + 1, tiles - 1))
        return carry

    @pl.when(tiles > 0)
    def _():
        p_sc[...] = jnp.zeros_like(p_sc)
        alpha_sc[...] = jnp.ones_like(alpha_sc)
        score(0)
        lax.fori_loop(0, tiles, step, 0)
        gather(tiles - 1)

    for g in range(groups):
        acc_ref[g, TOP:] = jnp.broadcast_to(m_sc[g], (AUG - TOP, WIDTH))


def attend(me, sides, qts, state, blocks, places, start=0, fresh=0, pooled=1):
    count, groups = len(blocks), len(sides) * GROUPS
    return pl.pallas_call(
        functools.partial(blocks_kernel, sides, start, fresh, pooled, places),
        out_shape=(
            jax.ShapeDtypeStruct((groups, AUG, WIDTH), F32),
            *[jax.ShapeDtypeStruct((count, BEAC, 2 * HEAD), BF16)] * pooled,
        ),
        in_specs=[
            pl.BlockSpec(memory_space=pltpu.SMEM),
            *[QT_SPEC] * len(sides),
            whole(*state.shape),
            *[whole(ROWS, 2 * HEAD)] * count,
        ],
        out_specs=(whole(groups, AUG, WIDTH), *[whole(count, BEAC, 2 * HEAD)] * pooled),
        scratch_shapes=[
            pltpu.VMEM((groups, HEAD, WIDTH), BF16),
            pltpu.VMEM((groups, 1, WIDTH), F32),
            pltpu.VMEM((count, TOK, HEAD), BF16),
            pltpu.VMEM((count, AUG, TOK), BF16),
            pltpu.VMEM((TOK, WIDTH), F32),
            pltpu.VMEM((TOK, WIDTH), BF16),
            pltpu.VMEM((1, WIDTH), F32),
            pltpu.VMEM((1, WIDTH), F32),
            pltpu.SMEM((count * groups + 1,), jnp.int32),
        ],
        cost_estimate=cost(count * len(sides)),
        compiler_params=PARAMS,
        name="attend",
    )(me, *qts, state, *blocks)


def final_kernel(counts, places, me_ref, q_ref, qt_ref, local_ref, mine_ref, sent_ref, *refs):
    beacon_refs = refs[: len(counts)]
    gap_ref, grads_ref, kb_sc, vb_sc, vt_sc, s_sc, p_sc, grad_sc, gap_sc = refs[len(counts) :]
    me = me_ref[0]
    kb_sc[...] = jnp.zeros_like(kb_sc)
    vb_sc[...] = jnp.zeros_like(vb_sc)
    n = 0
    for ref, count in zip(beacon_refs, counts):
        for i in range(count):
            at = pl.multiple_of(placed(me, *places[n]) * BEAC, BEAC)
            kb_sc[pl.ds(at, BEAC), :] = ref[i, :, 0:HEAD]
            vb_sc[pl.ds(at, BEAC), :] = ref[i, :, HEAD:]
            n += 1
    kb = kb_sc[...]
    vb = vb_sc[...]
    vt_sc[0:HEAD, :] = vb.T
    vt_sc[HEAD:, :] = jnp.ones((AUG - HEAD, SEQ * BEAC), BF16)
    seen = lax.broadcasted_iota(jnp.int32, (SEQ * BEAC, TOK), 0) < me * BEAC
    tops = []
    for h in range(HEADS):
        g, at = located(h)
        s = jnp.where(seen, dot(kb, qt_ref[g, :, at]), -1e30)
        s_sc[h] = s
        old = local_ref[g, TOP : TOP + 1, at]
        tops.append(jnp.maximum(old, jnp.max(s, axis=0, keepdims=True) * C2))
    for h in range(HEADS):
        p_sc[h] = jnp.exp2(s_sc[h] * C2 - tops[h]).astype(BF16)
    scaled = []
    for h in range(HEADS):
        g, at = located(h)
        old = jnp.exp2(local_ref[g, TOP : TOP + 1, at] - tops[h])
        student = local_ref[g, :, at] * old + dot(vt_sc[...], p_sc[h])
        inverse = 1.0 / student[SUM : SUM + 1, :]
        student = student[0:HEAD, :] * inverse
        old, new = mine_ref[g, TOP : TOP + 1, at], sent_ref[g, TOP : TOP + 1, at]
        top = jnp.maximum(old, new)
        old, new = jnp.exp2(old - top), jnp.exp2(new - top)
        total = mine_ref[g, SUM : SUM + 1, at] * old + sent_ref[g, SUM : SUM + 1, at] * new
        total = 1.0 / total
        teacher = mine_ref[g, 0:HEAD, at] * (old * total) + sent_ref[g, 0:HEAD, at] * (new * total)
        gap_t = (student - teacher).astype(BF16)
        gap_ref[:, span(h, HEAD)] = gap_t.T
        gap_t = gap_t.astype(F32) * inverse
        row_dot = jnp.sum(gap_t * student, axis=0, keepdims=True)
        gap_t = gap_t.astype(BF16)
        gap_sc[h] = gap_t.T
        scaled.append((gap_t, row_dot))
    for h in range(HEADS):
        gap_t, row_dot = scaled[h]
        grad_sc[h] = (p_sc[h].astype(F32) * (dot(vb, gap_t) - row_dot)).astype(BF16)
    grad_keys = dot(grad_sc[0], q_ref[:, span(0, HEAD)])
    grad_values = dot(p_sc[0], gap_sc[0])
    for h in range(1, HEADS):
        grad_keys = grad_keys + dot(grad_sc[h], q_ref[:, span(h, HEAD)])
        grad_values = grad_values + dot(p_sc[h], gap_sc[h])
    grads_ref[:, 0:HEAD] = (grad_keys * SCALE).astype(BF16)
    grads_ref[:, HEAD:] = grad_values.astype(BF16)


def finish(me, queries, qt, states, beacons, places):
    counts = [b.shape[0] for b in beacons]
    return pl.pallas_call(
        functools.partial(final_kernel, counts, places),
        out_shape=(
            jax.ShapeDtypeStruct((TOK, HEADS * HEAD), BF16),
            jax.ShapeDtypeStruct((SEQ * BEAC, 2 * HEAD), BF16),
        ),
        in_specs=[
            pl.BlockSpec(memory_space=pltpu.SMEM),
            whole(TOK, HEADS * HEAD),
            QT_SPEC,
            *[STATE_SPEC] * len(states),
            *[whole(*b.shape) for b in beacons],
        ],
        out_specs=(whole(TOK, HEADS * HEAD), whole(SEQ * BEAC, 2 * HEAD)),
        scratch_shapes=[
            pltpu.VMEM((SEQ * BEAC, HEAD), BF16),
            pltpu.VMEM((SEQ * BEAC, HEAD), BF16),
            pltpu.VMEM((AUG, SEQ * BEAC), BF16),
            pltpu.VMEM((HEADS, SEQ * BEAC, TOK), F32),
            pltpu.VMEM((HEADS, SEQ * BEAC, TOK), BF16),
            pltpu.VMEM((HEADS, SEQ * BEAC, TOK), BF16),
            pltpu.VMEM((HEADS, TOK, HEAD), BF16),
        ],
        cost_estimate=cost(2),
        compiler_params=PARAMS,
        name="finish",
    )(me, queries, qt, *states, *beacons)


def moved(block, dx, dy, dc):
    return lax.ppermute(block, "seq", [(s, placed(s, dx, dy, dc)) for s in range(SEQ)])


def swapped(block):
    return moved(block, 0, 0, 1)


def layer(queries, teacher_keys, teacher_values, beacon_starts):
    me = lax.axis_index("seq").reshape(1)
    own = prep(beacon_starts, teacher_keys, teacher_values)
    left = moved(own, 1, 0, 0)
    across = moved(own, 0, 1, 0)
    right = moved(own, 3, 0, 0)
    qt, state_local = local(queries, teacher_keys, teacher_values)
    qt_twin = swapped(qt)
    opposite = moved(own, 2, 1, 0)
    left2 = moved(left, 1, 0, 0)
    left_across = moved(left, 0, 1, 0)
    right_across = moved(across, 3, 0, 0)
    near = [own, left, across, right]
    near_places = [(0, 0, 0), (3, 0, 0), (0, 1, 0), (1, 0, 0)]
    far = [left2, left_across, right_across, opposite]
    far_places = [(2, 0, 0), (3, 1, 0), (1, 1, 0), (2, 1, 0)]
    state, near_rows = attend(
        me, (0, 1), (qt, qt_twin), state_local, near, near_places, fresh=GROUPS
    )
    near_twin = swapped(near_rows)
    lent, far_rows = attend(me, (1,), (qt_twin,), state, far, far_places, start=GROUPS)
    sent = swapped(lent)
    far_twin = swapped(far_rows)
    (mine,) = attend(me, (0,), (qt,), state, far, far_places, pooled=0)
    places = near_places + far_places
    places = places + [(dx, dy, 1) for dx, dy, _ in places]
    gap, grads = finish(
        me,
        queries,
        qt,
        (state_local, mine, sent),
        (near_rows, far_rows, near_twin, far_twin),
        places,
    )
    arrived = lax.all_to_all(grads.reshape(SEQ, BEAC, 2 * HEAD), "seq", 0, 0, tiled=True)
    key_rows, value_rows = (
        jnp.sum(part.astype(F32), axis=0) for part in jnp.split(arrived, 2, axis=2)
    )
    return gap, key_rows, value_rows


def solution(mesh):
    spec = P(("doc", "seq"), None)
    return jax.shard_map(
        layer,
        mesh=mesh,
        in_specs=(spec, spec, spec, P(("doc", "seq"))),
        out_specs=(spec, spec, spec),
        check_vma=False,
    )
```

profile of v0, /device:TPU:1, one launch (start us, length us, event | category | flops | bytes accessed | tf_op | source)
XLA Modules:
  0.0 71.6 jit_solution(3778685455824640975)
XLA Ops:
  0.6 3.2 %local.1 = (bf16[2,128,1024]{2,1,0:T(8,128)(2,1)S(1)}, f32[2,144,1024]{2,1,0:T(8,128)S(1)}) custom-call(bf16[512,512]{1,0:T(8,128)(2,1)} %q_ref.1, bf16[512,128]{1,0:T(8,128)(2,1)} %keys_ref.3, bf16[512,128]{1,0:T(8,128)(2,1)} %values_ref.3), custom_call_target="tpu_custom_call" | custom-call | flops 536870912 | bytes 1048576 | tf_op jit(solution)/shard_map/local/pallas_call | solution.py:128
  3.9 3.3 %collective-permute-start = (bf16[2,128,1024]{2,1,0:T(8,128)(2,1)S(1)}, bf16[2,128,1024]{2,1,0:T(8,128)(2,1)S(1)}, u32[]{:S(2)}, u32[]{:S(2)}) collective-permute-start(bf16[2,128,1024]{2,1,0:T(8,128)(2,1)S(1)} %get-tuple-element.11.refs_0_.qt_ref), channel_id=1, source_target_pairs={{0,1},{1,0},{2,3},{3,2},{4,5},{5,4},{6,7},{7,6},{8,9},{9,8},{10,11... | collective-permute-start | bytes 1572872 | tf_op jit(solution)/shard_map/ppermute | solution.py:335
  7.2 1.2 %prep.1.refs_3_ = bf16[544,256]{1,0:T(8,128)(2,1)S(1)} custom-call(s32[32]{0:T(128)} %starts_ref.1, bf16[512,128]{1,0:T(8,128)(2,1)} %keys_ref.3, bf16[512,128]{1,0:T(8,128)(2,1)} %values_ref.3), custom_call_target="tpu_custom_call" | custom-call | tf_op jit(solution)/shard_map/prep/pallas_call | solution.py:57
  8.4 0.1 collective-permute-start.1
  8.5 2.7 %collective-permute-start.3 = (bf16[544,256]{1,0:T(8,128)(2,1)S(1)}, bf16[544,256]{1,0:T(8,128)(2,1)}, u32[]{:S(2)}, u32[]{:S(2)}) collective-permute-start(bf16[544,256]{1,0:T(8,128)(2,1)S(1)} %prep.1.refs_3_), channel_id=1, source_target_pairs={{0,12},{1,13},{2,14},{3,15},{4,0},{5,1},{6,2},{7,3},{8,4},{9,5},{1... | collective-permute-start | bytes 835592 | tf_op jit(solution)/shard_map/ppermute | solution.py:335
  11.2 1.2 %collective-permute-start.2 = (bf16[544,256]{1,0:T(8,128)(2,1)S(1)}, bf16[544,256]{1,0:T(8,128)(2,1)S(1)}, u32[]{:S(2)}, u32[]{:S(2)}) collective-permute-start(bf16[544,256]{1,0:T(8,128)(2,1)S(1)} %prep.1.refs_3_), channel_id=1, source_target_pairs={{0,2},{1,3},{2,0},{3,1},{4,6},{5,7},{6,4},{7,5},{8,10},{9,11},{10,... | collective-permute-start | bytes 835592 | tf_op jit(solution)/shard_map/ppermute | solution.py:335
  12.4 1.3 %collective-permute-start.7 = (bf16[544,256]{1,0:T(8,128)(2,1)S(1)}, bf16[544,256]{1,0:T(8,128)(2,1)S(1)}, u32[]{:S(2)}, u32[]{:S(2)}) collective-permute-start(bf16[544,256]{1,0:T(8,128)(2,1)S(1)} %prep.1.refs_3_), channel_id=1, source_target_pairs={{0,10},{1,11},{2,8},{3,9},{4,14},{5,15},{6,12},{7,13},{8,2},{9,3},... | collective-permute-start | bytes 835592 | tf_op jit(solution)/shard_map/ppermute | solution.py:335
  13.7 4.2 %collective-permute-done.1.refs_4_ = bf16[544,256]{1,0:T(8,128)(2,1)S(1)} collective-permute-done((bf16[544,256]{1,0:T(8,128)(2,1)S(1)}, bf16[544,256]{1,0:T(8,128)(2,1)S(1)}, u32[]{:S(2)}, u32[]{:S(2)}) %collective-permute-start.1) | collective-permute-done | bytes 278560 | tf_op jit(solution)/shard_map/ppermute | solution.py:335
  17.9 1.2 %collective-permute-start.5 = (bf16[544,256]{1,0:T(8,128)(2,1)S(1)}, bf16[544,256]{1,0:T(8,128)(2,1)S(1)}, u32[]{:S(2)}, u32[]{:S(2)}) collective-permute-start(bf16[544,256]{1,0:T(8,128)(2,1)S(1)} %collective-permute-done.1.refs_4_), channel_id=1, source_target_pairs={{0,2},{1,3},{2,0},{3,1},{4,6},{5,7},{6,4},{7,5},{8,10},{9,11},{10,... | collective-permute-start | bytes 835592 | tf_op jit(solution)/shard_map/ppermute | solution.py:335
  19.1 3.6 %collective-permute-done.3.refs_6_ = bf16[544,256]{1,0:T(8,128)(2,1)} collective-permute-done((bf16[544,256]{1,0:T(8,128)(2,1)S(1)}, bf16[544,256]{1,0:T(8,128)(2,1)}, u32[]{:S(2)}, u32[]{:S(2)}) %collective-permute-start.3) | collective-permute-done | bytes 278560 | tf_op jit(solution)/shard_map/ppermute | solution.py:335
  22.7 0.0 collective-permute-start.4
  22.7 0.9 %collective-permute-done.2.refs_5_ = bf16[544,256]{1,0:T(8,128)(2,1)S(1)} collective-permute-done((bf16[544,256]{1,0:T(8,128)(2,1)S(1)}, bf16[544,256]{1,0:T(8,128)(2,1)S(1)}, u32[]{:S(2)}, u32[]{:S(2)}) %collective-permute-start.2) | collective-permute-done | bytes 278560 | tf_op jit(solution)/shard_map/ppermute | solution.py:335
  23.6 2.7 %collective-permute-start.6 = (bf16[544,256]{1,0:T(8,128)(2,1)S(1)}, bf16[544,256]{1,0:T(8,128)(2,1)S(1)}, u32[]{:S(2)}, u32[]{:S(2)}) collective-permute-start(bf16[544,256]{1,0:T(8,128)(2,1)S(1)} %collective-permute-done.2.refs_5_), channel_id=1, source_target_pairs={{0,12},{1,13},{2,14},{3,15},{4,0},{5,1},{6,2},{7,3},{8,4},{9,5},{1... | collective-permute-start | bytes 835592 | tf_op jit(solution)/shard_map/ppermute | solution.py:335
  26.4 0.0 collective-permute-done.refs_1_.refs_0_
  26.4 1.5 %attend.3 = (f32[4,144,1024]{2,1,0:T(8,128)S(1)}, bf16[4,32,256]{2,1,0:T(8,128)(2,1)S(1)}) custom-call(s32[1]{0:T(128)} %bitcast.me_ref, bf16[2,128,1024]{2,1,0:T(8,128)(2,1)S(1)} %get-tuple-element.11.refs_0_.qt_ref, bf16[2,128,1024]{2,1,0:T(8,128)(2,1)S(1)} %collective-permute-done.refs_1_.refs_0_, ...), custom_call_target="tpu_custom_call" | custom-call | flops 4294967296 | bytes 1048576 | tf_op jit(solution)/shard_map/attend/pallas_call | solution.py:214
  27.8 0.0 collective-permute-done.7.refs_5_
  27.8 2.5 %collective-permute-done.6.refs_4_ = bf16[544,256]{1,0:T(8,128)(2,1)S(1)} collective-permute-done((bf16[544,256]{1,0:T(8,128)(2,1)S(1)}, bf16[544,256]{1,0:T(8,128)(2,1)S(1)}, u32[]{:S(2)}, u32[]{:S(2)}) %collective-permute-start.6) | collective-permute-done | bytes 278560 | tf_op jit(solution)/shard_map/ppermute | solution.py:335
  30.4 0.8 %collective-permute-done.5.refs_3_ = bf16[544,256]{1,0:T(8,128)(2,1)S(1)} collective-permute-done((bf16[544,256]{1,0:T(8,128)(2,1)S(1)}, bf16[544,256]{1,0:T(8,128)(2,1)S(1)}, u32[]{:S(2)}, u32[]{:S(2)}) %collective-permute-start.5) | collective-permute-done | bytes 278560 | tf_op jit(solution)/shard_map/ppermute | solution.py:335
  31.2 0.9 %collective-permute-done.4.refs_2_ = bf16[544,256]{1,0:T(8,128)(2,1)S(1)} collective-permute-done((bf16[544,256]{1,0:T(8,128)(2,1)S(1)}, bf16[544,256]{1,0:T(8,128)(2,1)S(1)}, u32[]{:S(2)}, u32[]{:S(2)}) %collective-permute-start.4) | collective-permute-done | bytes 278560 | tf_op jit(solution)/shard_map/ppermute | solution.py:335
  32.1 0.3 attend.5
  32.4 3.3 %collective-permute-start.8 = (f32[2,144,1024]{2,1,0:T(8,128)S(1)}, f32[2,144,1024]{2,1,0:T(8,128)S(1)}, u32[]{:S(2)}, u32[]{:S(2)}) collective-permute-start(f32[2,144,1024]{2,1,0:T(8,128)S(1)} %get-tuple-element.14), channel_id=1, source_target_pairs={{0,1},{1,0},{2,3},{3,2},{4,5},{5,4},{6,7},{7,6},{8,9},{9,8},{10,11... | collective-permute-start | bytes 3538952 | tf_op jit(solution)/shard_map/ppermute | solution.py:335
  35.6 0.1 collective-permute-start.9
  35.7 0.0 copy-start
  35.7 0.4 collective-permute-start.10
  36.2 0.3 attend.4.mine_ref
  36.5 1.7 %collective-permute-done.9.refs_2_ = bf16[4,32,256]{2,1,0:T(8,128)(2,1)S(1)} collective-permute-done((bf16[4,32,256]{2,1,0:T(8,128)(2,1)S(1)}, bf16[4,32,256]{2,1,0:T(8,128)(2,1)S(1)}, u32[]{:S(2)}, u32[]{:S(2)}) %collective-permute-start.9) | collective-permute-done | bytes 65568 | tf_op jit(solution)/shard_map/ppermute | solution.py:335
  38.2 0.1 collective-permute-done.10.refs_3_
  38.3 0.0 collective-permute-done.8.sent_ref
  38.3 0.0 copy-done
  38.3 4.6 %finish.1 = (bf16[512,512]{1,0:T(8,128)(2,1)}, bf16[512,256]{1,0:T(8,128)(2,1)S(1)}) custom-call(s32[1]{0:T(128)} %bitcast.me_ref, bf16[512,512]{1,0:T(8,128)(2,1)S(1)} %copy-done, bf16[2,128,1024]{2,1,0:T(8,128)(2,1)S(1)} %get-tuple-element.11.refs_0_.qt_ref, f32[2,144,1024]{2,1,0:T(8,128)S(1)} %get-tuple-element.12.refs_2_.local_ref, ...), custom_call_target="tpu_custom_call" | custom-call | flops 1073741824 | bytes 1048576 | tf_op jit(solution)/shard_map/finish/pallas_call | solution.py:305
  42.9 28.0 %all_to_all.5 = bf16[16,32,256]{2,1,0:T(8,128)(2,1)S(1)} all-to-all(bf16[16,32,256]{2,1,0:T(8,128)(2,1)S(1)} %bitcast.2), channel_id=1, replica_groups=mesh['doc'=16,'seq'=16] {'seq'}, dimensions={0} | all-to-all | bytes 524288 | tf_op jit(solution)/shard_map/all_to_all | solution.py:376
  70.9 0.6 convert_reduce_fusion
Async XLA Ops:
  3.9 22.5 %collective-permute-start = (bf16[2,128,1024]{2,1,0:T(8,128)(2,1)S(1)}, bf16[2,128,1024]{2,1,0:T(8,128)(2,1)S(1)}, u32[]{:S(2)}, u32[]{:S(2)}) collective-permute-start(bf16[2,128,1024]{2,1,0:T(8,128)(2,1)S(1)} %get-tuple-element.11.refs_0_.qt_ref), channel_id=1, source_target_pairs={{0,1},{1,0},{2,3},{3,2},{4,5},{5,4},{6,7},{7,6},{8,9},{9,8},{10,11... | collective-permute-start | bytes 1572872 | tf_op jit(solution)/shard_map/ppermute | solution.py:335
  8.4 9.5 %collective-permute-start.1 = (bf16[544,256]{1,0:T(8,128)(2,1)S(1)}, bf16[544,256]{1,0:T(8,128)(2,1)S(1)}, u32[]{:S(2)}, u32[]{:S(2)}) collective-permute-start(bf16[544,256]{1,0:T(8,128)(2,1)S(1)} %prep.1.refs_3_), channel_id=1, source_target_pairs={{0,4},{1,5},{2,6},{3,7},{4,8},{5,9},{6,10},{7,11},{8,12},{9,13},{1... | collective-permute-start | bytes 835592 | tf_op jit(solution)/shard_map/ppermute | solution.py:335
  8.5 14.2 %collective-permute-start.3 = (bf16[544,256]{1,0:T(8,128)(2,1)S(1)}, bf16[544,256]{1,0:T(8,128)(2,1)}, u32[]{:S(2)}, u32[]{:S(2)}) collective-permute-start(bf16[544,256]{1,0:T(8,128)(2,1)S(1)} %prep.1.refs_3_), channel_id=1, source_target_pairs={{0,12},{1,13},{2,14},{3,15},{4,0},{5,1},{6,2},{7,3},{8,4},{9,5},{1... | collective-permute-start | bytes 835592 | tf_op jit(solution)/shard_map/ppermute | solution.py:335
  11.2 12.5 %collective-permute-start.2 = (bf16[544,256]{1,0:T(8,128)(2,1)S(1)}, bf16[544,256]{1,0:T(8,128)(2,1)S(1)}, u32[]{:S(2)}, u32[]{:S(2)}) collective-permute-start(bf16[544,256]{1,0:T(8,128)(2,1)S(1)} %prep.1.refs_3_), channel_id=1, source_target_pairs={{0,2},{1,3},{2,0},{3,1},{4,6},{5,7},{6,4},{7,5},{8,10},{9,11},{10,... | collective-permute-start | bytes 835592 | tf_op jit(solution)/shard_map/ppermute | solution.py:335
  12.4 15.5 %collective-permute-start.7 = (bf16[544,256]{1,0:T(8,128)(2,1)S(1)}, bf16[544,256]{1,0:T(8,128)(2,1)S(1)}, u32[]{:S(2)}, u32[]{:S(2)}) collective-permute-start(bf16[544,256]{1,0:T(8,128)(2,1)S(1)} %prep.1.refs_3_), channel_id=1, source_target_pairs={{0,10},{1,11},{2,8},{3,9},{4,14},{5,15},{6,12},{7,13},{8,2},{9,3},... | collective-permute-start | bytes 835592 | tf_op jit(solution)/shard_map/ppermute | solution.py:335
  17.9 13.3 %collective-permute-start.5 = (bf16[544,256]{1,0:T(8,128)(2,1)S(1)}, bf16[544,256]{1,0:T(8,128)(2,1)S(1)}, u32[]{:S(2)}, u32[]{:S(2)}) collective-permute-start(bf16[544,256]{1,0:T(8,128)(2,1)S(1)} %collective-permute-done.1.refs_4_), channel_id=1, source_target_pairs={{0,2},{1,3},{2,0},{3,1},{4,6},{5,7},{6,4},{7,5},{8,10},{9,11},{10,... | collective-permute-start | bytes 835592 | tf_op jit(solution)/shard_map/ppermute | solution.py:335
  22.7 9.4 %collective-permute-start.4 = (bf16[544,256]{1,0:T(8,128)(2,1)S(1)}, bf16[544,256]{1,0:T(8,128)(2,1)S(1)}, u32[]{:S(2)}, u32[]{:S(2)}) collective-permute-start(bf16[544,256]{1,0:T(8,128)(2,1)S(1)} %collective-permute-done.1.refs_4_), channel_id=1, source_target_pairs={{0,4},{1,5},{2,6},{3,7},{4,8},{5,9},{6,10},{7,11},{8,12},{9,13},{1... | collective-permute-start | bytes 835592 | tf_op jit(solution)/shard_map/ppermute | solution.py:335
  23.6 6.7 %collective-permute-start.6 = (bf16[544,256]{1,0:T(8,128)(2,1)S(1)}, bf16[544,256]{1,0:T(8,128)(2,1)S(1)}, u32[]{:S(2)}, u32[]{:S(2)}) collective-permute-start(bf16[544,256]{1,0:T(8,128)(2,1)S(1)} %collective-permute-done.2.refs_5_), channel_id=1, source_target_pairs={{0,12},{1,13},{2,14},{3,15},{4,0},{5,1},{6,2},{7,3},{8,4},{9,5},{1... | collective-permute-start | bytes 835592 | tf_op jit(solution)/shard_map/ppermute | solution.py:335
  32.4 5.9 %collective-permute-start.8 = (f32[2,144,1024]{2,1,0:T(8,128)S(1)}, f32[2,144,1024]{2,1,0:T(8,128)S(1)}, u32[]{:S(2)}, u32[]{:S(2)}) collective-permute-start(f32[2,144,1024]{2,1,0:T(8,128)S(1)} %get-tuple-element.14), channel_id=1, source_target_pairs={{0,1},{1,0},{2,3},{3,2},{4,5},{5,4},{6,7},{7,6},{8,9},{9,8},{10,11... | collective-permute-start | bytes 3538952 | tf_op jit(solution)/shard_map/ppermute | solution.py:335
  35.6 2.6 %collective-permute-start.9 = (bf16[4,32,256]{2,1,0:T(8,128)(2,1)S(1)}, bf16[4,32,256]{2,1,0:T(8,128)(2,1)S(1)}, u32[]{:S(2)}, u32[]{:S(2)}) collective-permute-start(bf16[4,32,256]{2,1,0:T(8,128)(2,1)S(1)} %get-tuple-element.15.refs_0_), channel_id=1, source_target_pairs={{0,1},{1,0},{2,3},{3,2},{4,5},{5,4},{6,7},{7,6},{8,9},{9,8},{10,11... | collective-permute-start | bytes 196616 | tf_op jit(solution)/shard_map/ppermute | solution.py:335
  35.7 2.6 %copy-start = (bf16[512,512]{1,0:T(8,128)(2,1)S(1)}, bf16[512,512]{1,0:T(8,128)(2,1)}, u32[]{:S(2)}) copy-start(bf16[512,512]{1,0:T(8,128)(2,1)} %q_ref.1) | copy-start | bytes 1572868
  35.7 2.6 %collective-permute-start.10 = (bf16[4,32,256]{2,1,0:T(8,128)(2,1)S(1)}, bf16[4,32,256]{2,1,0:T(8,128)(2,1)S(1)}, u32[]{:S(2)}, u32[]{:S(2)}) collective-permute-start(bf16[4,32,256]{2,1,0:T(8,128)(2,1)S(1)} %get-tuple-element.16.refs_1_), channel_id=1, source_target_pairs={{0,1},{1,0},{2,3},{3,2},{4,5},{5,4},{6,7},{7,6},{8,9},{9,8},{10,11... | collective-permute-start | bytes 196616 | tf_op jit(solution)/shard_map/ppermute | solution.py:335
where the time goes:
time: 71.8 us; the launch traced here: 71.6 us
  blocking collectives  28 us (39%)
  starting transfers between devices  16.3 us (23%)
  waiting for transfers between devices  14.8 us (21%)
  Pallas kernels  11.2 us (16%)
    all_to_all x1, blocking collectives, layer(): lax.all_to_all(grads.reshape(SEQ, BEAC, 2 * HEAD), 'seq', 0, 0, tiled=True)  28 us
    ppermute x11, starting transfers between devices, moved(): lax.ppermute(block, 'seq', [(s, placed(s, dx, dy, dc)) for s in range(SEQ)])  16.3 us
    ppermute x11, waiting for transfers between devices, moved(): lax.ppermute(block, 'seq', [(s, placed(s, dx, dy, dc)) for s in range(SEQ)])  14.8 us
    pallas_call x1, Pallas kernels, finish(): pl.pallas_call(functools.partial(final_kernel, counts, places), out_shape...  4.6 us
    pallas_call x1, Pallas kernels, local(): pl.pallas_call(local_kernel, out_shape=(QT_SHAPE, STATE), in_specs=[whole...  3.25 us
    pallas_call x3, Pallas kernels, attend(): pl.pallas_call(functools.partial(blocks_kernel, sides, start, fresh, pool...  2.11 us
  transfers between devices with their start and end apart: 11, of which 8 were waited for; matrix products, arithmetic and copies ran while one was open for 0% of the time, Pallas kernels for 4%

commit v1 on v0

--- a/solution.py
+++ b/solution.py
@@ -137,10 +137,10 @@
     )(*[pltpu.with_memory_space_constraint(a, pltpu.HBM) for a in (queries, keys, values)])
 
 
-def blocks_kernel(sides, start, fresh, pooled, places, me_ref, *refs):
+def blocks_kernel(sides, start, fresh, pooled, places, *refs):
     count = len(places)
     groups = len(sides) * GROUPS
-    me = me_ref[0]
+    me = lax.axis_index("seq")
     qt_refs, refs = refs[: len(sides)], refs[len(sides) :]
     in_ref, refs = refs[0], refs[1:]
     block_refs, refs = refs[:count], refs[count:]
@@ -158,16 +158,12 @@
             m_sc[g] = jnp.full((1, WIDTH), -1e30, F32)
     tiles = jnp.int32(0)
     for i in range(count):
-        k_sc[i] = block_refs[i][0:TOK, 0:HEAD]
-        vt_sc[i, 0:HEAD, :] = block_refs[i][0:TOK, HEAD:].T
-        vt_sc[i, HEAD:, :] = jnp.ones((AUG - HEAD, TOK), BF16)
-        if pooled:
-            beacons_ref[i] = block_refs[i][TOK:, :]
         for n, side in enumerate(sides):
             seen = (placed(me, *places[i]) < placed(me, 0, 0, side)).astype(jnp.int32)
             for g in range(GROUPS):
                 tile_ref[tiles] = i * groups + n * GROUPS + g
                 tiles = tiles + seen
+        k_sc[i] = block_refs[i][0:TOK, 0:HEAD]
 
     def where_is(t):
         tile = tile_ref[t]
@@ -192,24 +188,30 @@
         acc_ref[g] = acc_ref[g] * alpha_sc[...] + dot(vt_sc[i], p_sc[...])
 
     def step(t, carry):
-        gather(jnp.maximum(t - 1, 0))
+        gather(t - 1)
         weigh(t)
         score(jnp.minimum(t + 1, tiles - 1))
         return carry
 
+    score(0)
+    for i in range(count):
+        vt_sc[i, 0:HEAD, :] = block_refs[i][0:TOK, HEAD:].T
+        vt_sc[i, HEAD:, :] = jnp.ones((AUG - HEAD, TOK), BF16)
+        if pooled:
+            beacons_ref[i] = block_refs[i][TOK:, :]
+
     @pl.when(tiles > 0)
     def _():
-        p_sc[...] = jnp.zeros_like(p_sc)
-        alpha_sc[...] = jnp.ones_like(alpha_sc)
-        score(0)
-        lax.fori_loop(0, tiles, step, 0)
+        weigh(0)
+        score(1)
+        lax.fori_loop(1, tiles, step, 0)
         gather(tiles - 1)
 
     for g in range(groups):
         acc_ref[g, TOP:] = jnp.broadcast_to(m_sc[g], (AUG - TOP, WIDTH))
 
 
-def attend(me, sides, qts, state, blocks, places, start=0, fresh=0, pooled=1):
+def attend(sides, qts, state, blocks, places, start=0, fresh=0, pooled=1):
     count, groups = len(blocks), len(sides) * GROUPS
     return pl.pallas_call(
         functools.partial(blocks_kernel, sides, start, fresh, pooled, places),
@@ -218,7 +220,6 @@
             *[jax.ShapeDtypeStruct((count, BEAC, 2 * HEAD), BF16)] * pooled,
         ),
         in_specs=[
-            pl.BlockSpec(memory_space=pltpu.SMEM),
             *[QT_SPEC] * len(sides),
             whole(*state.shape),
             *[whole(ROWS, 2 * HEAD)] * count,
@@ -238,13 +239,13 @@
         cost_estimate=cost(count * len(sides)),
         compiler_params=PARAMS,
         name="attend",
-    )(me, *qts, state, *blocks)
-
-
-def final_kernel(counts, places, me_ref, q_ref, qt_ref, local_ref, mine_ref, sent_ref, *refs):
+    )(*qts, state, *blocks)
+
+
+def final_kernel(counts, places, q_ref, qt_ref, local_ref, mine_ref, sent_ref, *refs):
     beacon_refs = refs[: len(counts)]
-    gap_ref, grads_ref, kb_sc, vb_sc, vt_sc, s_sc, p_sc, grad_sc, gap_sc = refs[len(counts) :]
-    me = me_ref[0]
+    gap_hbm, grads_ref, gap_ref, kb_sc, vb_sc, vt_sc, s_sc, p_sc, grad_sc, gap_sc, sem = refs[len(counts) :]
+    me = lax.axis_index("seq")
     kb_sc[...] = jnp.zeros_like(kb_sc)
     vb_sc[...] = jnp.zeros_like(vb_sc)
     n = 0
@@ -288,6 +289,8 @@
         gap_t = gap_t.astype(BF16)
         gap_sc[h] = gap_t.T
         scaled.append((gap_t, row_dot))
+    gap_copy = pltpu.make_async_copy(gap_ref, gap_hbm, sem)
+    gap_copy.start()
     for h in range(HEADS):
         gap_t, row_dot = scaled[h]
         grad_sc[h] = (p_sc[h].astype(F32) * (dot(vb, gap_t) - row_dot)).astype(BF16)
@@ -298,25 +301,26 @@
         grad_values = grad_values + dot(p_sc[h], gap_sc[h])
     grads_ref[:, 0:HEAD] = (grad_keys * SCALE).astype(BF16)
     grads_ref[:, HEAD:] = grad_values.astype(BF16)
-
-
-def finish(me, queries, qt, states, beacons, places):
+    gap_copy.wait()
+
+
+def finish(queries, qt, states, beacons, places):
     counts = [b.shape[0] for b in beacons]
     return pl.pallas_call(
         functools.partial(final_kernel, counts, places),
         out_shape=(
             jax.ShapeDtypeStruct((TOK, HEADS * HEAD), BF16),
-            jax.ShapeDtypeStruct((SEQ * BEAC, 2 * HEAD), BF16),
+            pltpu.VMEM((SEQ * BEAC, 2 * HEAD), BF16),
         ),
         in_specs=[
-            pl.BlockSpec(memory_space=pltpu.SMEM),
             whole(TOK, HEADS * HEAD),
             QT_SPEC,
             *[STATE_SPEC] * len(states),
             *[whole(*b.shape) for b in beacons],
         ],
-        out_specs=(whole(TOK, HEADS * HEAD), whole(SEQ * BEAC, 2 * HEAD)),
+        out_specs=(pl.BlockSpec(memory_space=pl.ANY), whole(SEQ * BEAC, 2 * HEAD)),
         scratch_shapes=[
+            pltpu.VMEM((TOK, HEADS * HEAD), BF16),
             pltpu.VMEM((SEQ * BEAC, HEAD), BF16),
             pltpu.VMEM((SEQ * BEAC, HEAD), BF16),
             pltpu.VMEM((AUG, SEQ * BEAC), BF16),
@@ -324,11 +328,12 @@
             pltpu.VMEM((HEADS, SEQ * BEAC, TOK), BF16),
             pltpu.VMEM((HEADS, SEQ * BEAC, TOK), BF16),
             pltpu.VMEM((HEADS, TOK, HEAD), BF16),
+            pltpu.SemaphoreType.DMA,
         ],
         cost_estimate=cost(2),
         compiler_params=PARAMS,
         name="finish",
-    )(me, queries, qt, *states, *beacons)
+    )(queries, qt, *states, *beacons)
 
 
 def moved(block, dx, dy, dc):
@@ -340,7 +345,6 @@
 
 
 def layer(queries, teacher_keys, teacher_values, beacon_starts):
-    me = lax.axis_index("seq").reshape(1)
     own = prep(beacon_starts, teacher_keys, teacher_values)
     left = moved(own, 1, 0, 0)
     across = moved(own, 0, 1, 0)
@@ -356,17 +360,16 @@
     far = [left2, left_across, right_across, opposite]
     far_places = [(2, 0, 0), (3, 1, 0), (1, 1, 0), (2, 1, 0)]
     state, near_rows = attend(
-        me, (0, 1), (qt, qt_twin), state_local, near, near_places, fresh=GROUPS
+        (0, 1), (qt, qt_twin), state_local, near, near_places, fresh=GROUPS
     )
     near_twin = swapped(near_rows)
-    lent, far_rows = attend(me, (1,), (qt_twin,), state, far, far_places, start=GROUPS)
+    lent, far_rows = attend((1,), (qt_twin,), state, far, far_places, start=GROUPS)
     sent = swapped(lent)
     far_twin = swapped(far_rows)
-    (mine,) = attend(me, (0,), (qt,), state, far, far_places, pooled=0)
+    (mine,) = attend((0,), (qt,), state, far, far_places, pooled=0)
     places = near_places + far_places
     places = places + [(dx, dy, 1) for dx, dy, _ in places]
     gap, grads = finish(
-        me,
         queries,
         qt,
         (state_local, mine, sent),

time: 71.8 us -> 69.5 us (0.968)
  blocking collectives: 28 us -> 25.6 us
    all_to_all x1, blocking collectives: 28 us -> 25.6 us  [layer(): lax.all_to_all(grads.reshape(SEQ, BEAC, 2 * HEAD), 'seq', 0, 0, tiled=True)]
where the time goes in v1:
time: 69.5 us; the launch traced here: 69.4 us
  blocking collectives  25.6 us (37%)
  starting transfers between devices  16.4 us (24%)
  waiting for transfers between devices  15.1 us (22%)
  Pallas kernels  11 us (16%)
  between operations  0.71 us (1%)
    all_to_all x1, blocking collectives, layer(): lax.all_to_all(grads.reshape(SEQ, BEAC, 2 * HEAD), 'seq', 0, 0, tiled=True)  25.6 us
    ppermute x11, starting transfers between devices, moved(): lax.ppermute(block, 'seq', [(s, placed(s, dx, dy, dc)) for s in range(SEQ)])  16.4 us
    ppermute x11, waiting for transfers between devices, moved(): lax.ppermute(block, 'seq', [(s, placed(s, dx, dy, dc)) for s in range(SEQ)])  15.1 us
    pallas_call x1, Pallas kernels, finish(): pl.pallas_call(functools.partial(final_kernel, counts, places), out_shape...  4.53 us
    pallas_call x1, Pallas kernels, local(): pl.pallas_call(local_kernel, out_shape=(QT_SHAPE, STATE), in_specs=[whole...  3.25 us
    pallas_call x3, Pallas kernels, attend(): pl.pallas_call(functools.partial(blocks_kernel, sides, start, fresh, pool...  1.99 us
  transfers between devices with their start and end apart: 11, of which 8 were waited for; matrix products, arithmetic and copies ran while one was open for 0% of the time, Pallas kernels for 4%

profile of v1, /device:TPU:1, one launch (start us, length us, event | category | flops | bytes accessed | tf_op | source)
XLA Modules:
  0.0 69.4 jit_solution(16305260899466364402)
XLA Ops:
  0.6 3.2 %local.1 = (bf16[2,128,1024]{2,1,0:T(8,128)(2,1)S(1)}, f32[2,144,1024]{2,1,0:T(8,128)S(1)}) custom-call(bf16[512,512]{1,0:T(8,128)(2,1)} %q_ref.1, bf16[512,128]{1,0:T(8,128)(2,1)} %keys_ref.3, bf16[512,128]{1,0:T(8,128)(2,1)} %values_ref.3), custom_call_target="tpu_custom_call" | custom-call | flops 536870912 | bytes 1048576 | tf_op jit(solution)/shard_map/local/pallas_call | solution.py:128
  3.9 3.3 %collective-permute-start = (bf16[2,128,1024]{2,1,0:T(8,128)(2,1)S(1)}, bf16[2,128,1024]{2,1,0:T(8,128)(2,1)S(1)}, u32[]{:S(2)}, u32[]{:S(2)}) collective-permute-start(bf16[2,128,1024]{2,1,0:T(8,128)(2,1)S(1)} %get-tuple-element.11.refs_0_.qt_ref), channel_id=1, source_target_pairs={{0,1},{1,0},{2,3},{3,2},{4,5},{5,4},{6,7},{7,6},{8,9},{9,8},{10,11... | collective-permute-start | bytes 1572872 | tf_op jit(solution)/shard_map/ppermute | solution.py:340
  7.2 1.2 %prep.1.refs_3_ = bf16[544,256]{1,0:T(8,128)(2,1)S(1)} custom-call(s32[32]{0:T(128)} %starts_ref.1, bf16[512,128]{1,0:T(8,128)(2,1)} %keys_ref.3, bf16[512,128]{1,0:T(8,128)(2,1)} %values_ref.3), custom_call_target="tpu_custom_call" | custom-call | tf_op jit(solution)/shard_map/prep/pallas_call | solution.py:57
  8.4 0.1 collective-permute-start.1
  8.5 2.7 %collective-permute-start.3 = (bf16[544,256]{1,0:T(8,128)(2,1)S(1)}, bf16[544,256]{1,0:T(8,128)(2,1)S(1)}, u32[]{:S(2)}, u32[]{:S(2)}) collective-permute-start(bf16[544,256]{1,0:T(8,128)(2,1)S(1)} %prep.1.refs_3_), channel_id=1, source_target_pairs={{0,12},{1,13},{2,14},{3,15},{4,0},{5,1},{6,2},{7,3},{8,4},{9,5},{1... | collective-permute-start | bytes 835592 | tf_op jit(solution)/shard_map/ppermute | solution.py:340
  11.2 1.2 %collective-permute-start.2 = (bf16[544,256]{1,0:T(8,128)(2,1)S(1)}, bf16[544,256]{1,0:T(8,128)(2,1)S(1)}, u32[]{:S(2)}, u32[]{:S(2)}) collective-permute-start(bf16[544,256]{1,0:T(8,128)(2,1)S(1)} %prep.1.refs_3_), channel_id=1, source_target_pairs={{0,2},{1,3},{2,0},{3,1},{4,6},{5,7},{6,4},{7,5},{8,10},{9,11},{10,... | collective-permute-start | bytes 835592 | tf_op jit(solution)/shard_map/ppermute | solution.py:340
  12.4 1.3 %collective-permute-start.7 = (bf16[544,256]{1,0:T(8,128)(2,1)S(1)}, bf16[544,256]{1,0:T(8,128)(2,1)S(1)}, u32[]{:S(2)}, u32[]{:S(2)}) collective-permute-start(bf16[544,256]{1,0:T(8,128)(2,1)S(1)} %prep.1.refs_3_), channel_id=1, source_target_pairs={{0,10},{1,11},{2,8},{3,9},{4,14},{5,15},{6,12},{7,13},{8,2},{9,3},... | collective-permute-start | bytes 835592 | tf_op jit(solution)/shard_map/ppermute | solution.py:340
  13.7 4.2 %collective-permute-done.1.refs_4_ = bf16[544,256]{1,0:T(8,128)(2,1)S(1)} collective-permute-done((bf16[544,256]{1,0:T(8,128)(2,1)S(1)}, bf16[544,256]{1,0:T(8,128)(2,1)S(1)}, u32[]{:S(2)}, u32[]{:S(2)}) %collective-permute-start.1) | collective-permute-done | bytes 278560 | tf_op jit(solution)/shard_map/ppermute | solution.py:340
  17.9 1.2 %collective-permute-start.5 = (bf16[544,256]{1,0:T(8,128)(2,1)S(1)}, bf16[544,256]{1,0:T(8,128)(2,1)S(1)}, u32[]{:S(2)}, u32[]{:S(2)}) collective-permute-start(bf16[544,256]{1,0:T(8,128)(2,1)S(1)} %collective-permute-done.1.refs_4_), channel_id=1, source_target_pairs={{0,2},{1,3},{2,0},{3,1},{4,6},{5,7},{6,4},{7,5},{8,10},{9,11},{10,... | collective-permute-start | bytes 835592 | tf_op jit(solution)/shard_map/ppermute | solution.py:340
  19.1 3.6 %collective-permute-done.3.refs_6_ = bf16[544,256]{1,0:T(8,128)(2,1)S(1)} collective-permute-done((bf16[544,256]{1,0:T(8,128)(2,1)S(1)}, bf16[544,256]{1,0:T(8,128)(2,1)S(1)}, u32[]{:S(2)}, u32[]{:S(2)}) %collective-permute-start.3) | collective-permute-done | bytes 278560 | tf_op jit(solution)/shard_map/ppermute | solution.py:340
  22.7 0.0 collective-permute-start.4
  22.7 0.9 %collective-permute-done.2.refs_5_ = bf16[544,256]{1,0:T(8,128)(2,1)S(1)} collective-permute-done((bf16[544,256]{1,0:T(8,128)(2,1)S(1)}, bf16[544,256]{1,0:T(8,128)(2,1)S(1)}, u32[]{:S(2)}, u32[]{:S(2)}) %collective-permute-start.2) | collective-permute-done | bytes 278560 | tf_op jit(solution)/shard_map/ppermute | solution.py:340
  23.6 2.6 %collective-permute-start.6 = (bf16[544,256]{1,0:T(8,128)(2,1)S(1)}, bf16[544,256]{1,0:T(8,128)(2,1)S(1)}, u32[]{:S(2)}, u32[]{:S(2)}) collective-permute-start(bf16[544,256]{1,0:T(8,128)(2,1)S(1)} %collective-permute-done.2.refs_5_), channel_id=1, source_target_pairs={{0,12},{1,13},{2,14},{3,15},{4,0},{5,1},{6,2},{7,3},{8,4},{9,5},{1... | collective-permute-start | bytes 835592 | tf_op jit(solution)/shard_map/ppermute | solution.py:340
  26.3 0.0 collective-permute-done.refs_1_.refs_0_
  26.3 0.7 %attend.3 = (f32[4,144,1024]{2,1,0:T(8,128)S(1)}, bf16[4,32,256]{2,1,0:T(8,128)(2,1)S(1)}) custom-call(bf16[2,128,1024]{2,1,0:T(8,128)(2,1)S(1)} %get-tuple-element.11.refs_0_.qt_ref, bf16[2,128,1024]{2,1,0:T(8,128)(2,1)S(1)} %collective-permute-done.refs_1_.refs_0_, f32[2,144,1024]{2,1,0:T(8,128)S(1)} %get-tuple-element.12.refs_2_.local_ref, ...), custom_call_target="tpu_custom_call" | custom-call | flops 4294967296 | bytes 1048576 | tf_op jit(solution)/shard_map/attend/pallas_call | solution.py:216
  27.0 0.0 collective-permute-done.7.refs_5_
  27.0 3.1 %collective-permute-done.6.refs_4_ = bf16[544,256]{1,0:T(8,128)(2,1)S(1)} collective-permute-done((bf16[544,256]{1,0:T(8,128)(2,1)S(1)}, bf16[544,256]{1,0:T(8,128)(2,1)S(1)}, u32[]{:S(2)}, u32[]{:S(2)}) %collective-permute-start.6) | collective-permute-done | bytes 278560 | tf_op jit(solution)/shard_map/ppermute | solution.py:340
  30.1 1.0 %collective-permute-done.5.refs_3_ = bf16[544,256]{1,0:T(8,128)(2,1)S(1)} collective-permute-done((bf16[544,256]{1,0:T(8,128)(2,1)S(1)}, bf16[544,256]{1,0:T(8,128)(2,1)S(1)}, u32[]{:S(2)}, u32[]{:S(2)}) %collective-permute-start.5) | collective-permute-done | bytes 278560 | tf_op jit(solution)/shard_map/ppermute | solution.py:340
  31.2 0.7 collective-permute-done.4.refs_2_
  31.8 0.6 attend.5
  32.5 3.5 %collective-permute-start.8 = (f32[2,144,1024]{2,1,0:T(8,128)S(1)}, f32[2,144,1024]{2,1,0:T(8,128)S(1)}, u32[]{:S(2)}, u32[]{:S(2)}) collective-permute-start(f32[2,144,1024]{2,1,0:T(8,128)S(1)} %get-tuple-element.14), channel_id=1, source_target_pairs={{0,1},{1,0},{2,3},{3,2},{4,5},{5,4},{6,7},{7,6},{8,9},{9,8},{10,11... | collective-permute-start | bytes 3538952 | tf_op jit(solution)/shard_map/ppermute | solution.py:340
  35.9 0.1 collective-permute-start.9
  36.0 0.0 copy-start
  36.0 0.4 collective-permute-start.10
  36.5 0.6 attend.4.mine_ref
  37.1 1.4 %collective-permute-done.9.refs_2_ = bf16[4,32,256]{2,1,0:T(8,128)(2,1)S(1)} collective-permute-done((bf16[4,32,256]{2,1,0:T(8,128)(2,1)S(1)}, bf16[4,32,256]{2,1,0:T(8,128)(2,1)S(1)}, u32[]{:S(2)}, u32[]{:S(2)}) %collective-permute-start.9) | collective-permute-done | bytes 65568 | tf_op jit(solution)/shard_map/ppermute | solution.py:340
  38.5 0.1 collective-permute-done.10.refs_3_
  38.6 0.0 collective-permute-done.8.sent_ref
  38.6 0.0 copy-done
  38.6 4.5 %finish.1 = (bf16[512,512]{1,0:T(8,128)(2,1)}, bf16[512,256]{1,0:T(8,128)(2,1)S(1)}) custom-call(bf16[512,512]{1,0:T(8,128)(2,1)S(1)} %copy-done, bf16[2,128,1024]{2,1,0:T(8,128)(2,1)S(1)} %get-tuple-element.11.refs_0_.qt_ref, f32[2,144,1024]{2,1,0:T(8,128)S(1)} %get-tuple-element.12.refs_2_.local_ref, f32[2,144,1024]{2,1,0:T(8,128)S(1)} %attend.4.mine_ref, ...), custom_call_target="tpu_custom_call" | custom-call | flops 1073741824 | bytes 1048576 | tf_op jit(solution)/shard_map/finish/pallas_call | solution.py:309
  43.1 25.6 %all_to_all.5 = bf16[16,32,256]{2,1,0:T(8,128)(2,1)S(1)} all-to-all(bf16[16,32,256]{2,1,0:T(8,128)(2,1)S(1)} %bitcast.1), channel_id=1, replica_groups=mesh['doc'=16,'seq'=16] {'seq'}, dimensions={0} | all-to-all | bytes 524288 | tf_op jit(solution)/shard_map/all_to_all | solution.py:379
  68.7 0.6 convert_reduce_fusion
Async XLA Ops:
  3.9 22.4 %collective-permute-start = (bf16[2,128,1024]{2,1,0:T(8,128)(2,1)S(1)}, bf16[2,128,1024]{2,1,0:T(8,128)(2,1)S(1)}, u32[]{:S(2)}, u32[]{:S(2)}) collective-permute-start(bf16[2,128,1024]{2,1,0:T(8,128)(2,1)S(1)} %get-tuple-element.11.refs_0_.qt_ref), channel_id=1, source_target_pairs={{0,1},{1,0},{2,3},{3,2},{4,5},{5,4},{6,7},{7,6},{8,9},{9,8},{10,11... | collective-permute-start | bytes 1572872 | tf_op jit(solution)/shard_map/ppermute | solution.py:340
  8.4 9.5 %collective-permute-start.1 = (bf16[544,256]{1,0:T(8,128)(2,1)S(1)}, bf16[544,256]{1,0:T(8,128)(2,1)S(1)}, u32[]{:S(2)}, u32[]{:S(2)}) collective-permute-start(bf16[544,256]{1,0:T(8,128)(2,1)S(1)} %prep.1.refs_3_), channel_id=1, source_target_pairs={{0,4},{1,5},{2,6},{3,7},{4,8},{5,9},{6,10},{7,11},{8,12},{9,13},{1... | collective-permute-start | bytes 835592 | tf_op jit(solution)/shard_map/ppermute | solution.py:340
  8.5 14.2 %collective-permute-start.3 = (bf16[544,256]{1,0:T(8,128)(2,1)S(1)}, bf16[544,256]{1,0:T(8,128)(2,1)S(1)}, u32[]{:S(2)}, u32[]{:S(2)}) collective-permute-start(bf16[544,256]{1,0:T(8,128)(2,1)S(1)} %prep.1.refs_3_), channel_id=1, source_target_pairs={{0,12},{1,13},{2,14},{3,15},{4,0},{5,1},{6,2},{7,3},{8,4},{9,5},{1... | collective-permute-start | bytes 835592 | tf_op jit(solution)/shard_map/ppermute | solution.py:340
  11.2 12.5 %collective-permute-start.2 = (bf16[544,256]{1,0:T(8,128)(2,1)S(1)}, bf16[544,256]{1,0:T(8,128)(2,1)S(1)}, u32[]{:S(2)}, u32[]{:S(2)}) collective-permute-start(bf16[544,256]{1,0:T(8,128)(2,1)S(1)} %prep.1.refs_3_), channel_id=1, source_target_pairs={{0,2},{1,3},{2,0},{3,1},{4,6},{5,7},{6,4},{7,5},{8,10},{9,11},{10,... | collective-permute-start | bytes 835592 | tf_op jit(solution)/shard_map/ppermute | solution.py:340
  12.4 14.6 %collective-permute-start.7 = (bf16[544,256]{1,0:T(8,128)(2,1)S(1)}, bf16[544,256]{1,0:T(8,128)(2,1)S(1)}, u32[]{:S(2)}, u32[]{:S(2)}) collective-permute-start(bf16[544,256]{1,0:T(8,128)(2,1)S(1)} %prep.1.refs_3_), channel_id=1, source_target_pairs={{0,10},{1,11},{2,8},{3,9},{4,14},{5,15},{6,12},{7,13},{8,2},{9,3},... | collective-permute-start | bytes 835592 | tf_op jit(solution)/shard_map/ppermute | solution.py:340
  17.9 13.3 %collective-permute-start.5 = (bf16[544,256]{1,0:T(8,128)(2,1)S(1)}, bf16[544,256]{1,0:T(8,128)(2,1)S(1)}, u32[]{:S(2)}, u32[]{:S(2)}) collective-permute-start(bf16[544,256]{1,0:T(8,128)(2,1)S(1)} %collective-permute-done.1.refs_4_), channel_id=1, source_target_pairs={{0,2},{1,3},{2,0},{3,1},{4,6},{5,7},{6,4},{7,5},{8,10},{9,11},{10,... | collective-permute-start | bytes 835592 | tf_op jit(solution)/shard_map/ppermute | solution.py:340
  22.7 9.1 %collective-permute-start.4 = (bf16[544,256]{1,0:T(8,128)(2,1)S(1)}, bf16[544,256]{1,0:T(8,128)(2,1)S(1)}, u32[]{:S(2)}, u32[]{:S(2)}) collective-permute-start(bf16[544,256]{1,0:T(8,128)(2,1)S(1)} %collective-permute-done.1.refs_4_), channel_id=1, source_target_pairs={{0,4},{1,5},{2,6},{3,7},{4,8},{5,9},{6,10},{7,11},{8,12},{9,13},{1... | collective-permute-start | bytes 835592 | tf_op jit(solution)/shard_map/ppermute | solution.py:340
  23.6 6.5 %collective-permute-start.6 = (bf16[544,256]{1,0:T(8,128)(2,1)S(1)}, bf16[544,256]{1,0:T(8,128)(2,1)S(1)}, u32[]{:S(2)}, u32[]{:S(2)}) collective-permute-start(bf16[544,256]{1,0:T(8,128)(2,1)S(1)} %collective-permute-done.2.refs_5_), channel_id=1, source_target_pairs={{0,12},{1,13},{2,14},{3,15},{4,0},{5,1},{6,2},{7,3},{8,4},{9,5},{1... | collective-permute-start | bytes 835592 | tf_op jit(solution)/shard_map/ppermute | solution.py:340
  32.5 6.1 %collective-permute-start.8 = (f32[2,144,1024]{2,1,0:T(8,128)S(1)}, f32[2,144,1024]{2,1,0:T(8,128)S(1)}, u32[]{:S(2)}, u32[]{:S(2)}) collective-permute-start(f32[2,144,1024]{2,1,0:T(8,128)S(1)} %get-tuple-element.14), channel_id=1, source_target_pairs={{0,1},{1,0},{2,3},{3,2},{4,5},{5,4},{6,7},{7,6},{8,9},{9,8},{10,11... | collective-permute-start | bytes 3538952 | tf_op jit(solution)/shard_map/ppermute | solution.py:340
  35.9 2.6 %collective-permute-start.9 = (bf16[4,32,256]{2,1,0:T(8,128)(2,1)S(1)}, bf16[4,32,256]{2,1,0:T(8,128)(2,1)S(1)}, u32[]{:S(2)}, u32[]{:S(2)}) collective-permute-start(bf16[4,32,256]{2,1,0:T(8,128)(2,1)S(1)} %get-tuple-element.15.refs_0_), channel_id=1, source_target_pairs={{0,1},{1,0},{2,3},{3,2},{4,5},{5,4},{6,7},{7,6},{8,9},{9,8},{10,11... | collective-permute-start | bytes 196616 | tf_op jit(solution)/shard_map/ppermute | solution.py:340
  36.0 2.6 %copy-start = (bf16[512,512]{1,0:T(8,128)(2,1)S(1)}, bf16[512,512]{1,0:T(8,128)(2,1)}, u32[]{:S(2)}) copy-start(bf16[512,512]{1,0:T(8,128)(2,1)} %q_ref.1) | copy-start | bytes 1572868
  36.0 2.6 %collective-permute-start.10 = (bf16[4,32,256]{2,1,0:T(8,128)(2,1)S(1)}, bf16[4,32,256]{2,1,0:T(8,128)(2,1)S(1)}, u32[]{:S(2)}, u32[]{:S(2)}) collective-permute-start(bf16[4,32,256]{2,1,0:T(8,128)(2,1)S(1)} %get-tuple-element.16.refs_1_), channel_id=1, source_target_pairs={{0,1},{1,0},{2,3},{3,2},{4,5},{5,4},{6,7},{7,6},{8,9},{9,8},{10,11... | collective-permute-start | bytes 196616 | tf_op jit(solution)/shard_map/ppermute | solution.py:340

commit v2 on v1

--- a/solution.py
+++ b/solution.py
@@ -137,13 +137,15 @@
     )(*[pltpu.with_memory_space_constraint(a, pltpu.HBM) for a in (queries, keys, values)])
 
 
-def blocks_kernel(sides, start, fresh, pooled, places, *refs):
+def blocks_kernel(sides, start, fresh, pooled, before, places, *refs):
     count = len(places)
     groups = len(sides) * GROUPS
     me = lax.axis_index("seq")
     qt_refs, refs = refs[: len(sides)], refs[len(sides) :]
     in_ref, refs = refs[0], refs[1:]
     block_refs, refs = refs[:count], refs[count:]
+    if before:
+        before_ref, refs = refs[0], refs[1:]
     acc_ref, refs = refs[0], refs[1:]
     if pooled:
         beacons_ref, refs = refs[0], refs[1:]
@@ -198,7 +200,9 @@
         vt_sc[i, 0:HEAD, :] = block_refs[i][0:TOK, HEAD:].T
         vt_sc[i, HEAD:, :] = jnp.ones((AUG - HEAD, TOK), BF16)
         if pooled:
-            beacons_ref[i] = block_refs[i][TOK:, :]
+            beacons_ref[before + i] = block_refs[i][TOK:, :]
+    if before:
+        beacons_ref[0:before] = before_ref[...]
 
     @pl.when(tiles > 0)
     def _():
@@ -211,20 +215,23 @@
         acc_ref[g, TOP:] = jnp.broadcast_to(m_sc[g], (AUG - TOP, WIDTH))
 
 
-def attend(sides, qts, state, blocks, places, start=0, fresh=0, pooled=1):
+def attend(sides, qts, state, blocks, places, start=0, fresh=0, pooled=1, rows=()):
     count, groups = len(blocks), len(sides) * GROUPS
+    before = rows[0].shape[0] if rows else 0
+    rows_shape = (before + count, BEAC, 2 * HEAD)
     return pl.pallas_call(
-        functools.partial(blocks_kernel, sides, start, fresh, pooled, places),
+        functools.partial(blocks_kernel, sides, start, fresh, pooled, before, places),
         out_shape=(
             jax.ShapeDtypeStruct((groups, AUG, WIDTH), F32),
-            *[jax.ShapeDtypeStruct((count, BEAC, 2 * HEAD), BF16)] * pooled,
+            *[jax.ShapeDtypeStruct(rows_shape, BF16)] * pooled,
         ),
         in_specs=[
             *[QT_SPEC] * len(sides),
             whole(*state.shape),
             *[whole(ROWS, 2 * HEAD)] * count,
+            *[whole(*r.shape) for r in rows],
         ],
-        out_specs=(whole(groups, AUG, WIDTH), *[whole(count, BEAC, 2 * HEAD)] * pooled),
+        out_specs=(whole(groups, AUG, WIDTH), *[whole(*rows_shape)] * pooled),
         scratch_shapes=[
             pltpu.VMEM((groups, HEAD, WIDTH), BF16),
             pltpu.VMEM((groups, 1, WIDTH), F32),
@@ -239,7 +246,7 @@
         cost_estimate=cost(count * len(sides)),
         compiler_params=PARAMS,
         name="attend",
-    )(*qts, state, *blocks)
+    )(*qts, state, *blocks, *rows)
 
 
 def final_kernel(counts, places, q_ref, qt_ref, local_ref, mine_ref, sent_ref, *refs):
@@ -357,25 +364,24 @@
     right_across = moved(across, 3, 0, 0)
     near = [own, left, across, right]
     near_places = [(0, 0, 0), (3, 0, 0), (0, 1, 0), (1, 0, 0)]
-    far = [left2, left_across, right_across, opposite]
-    far_places = [(2, 0, 0), (3, 1, 0), (1, 1, 0), (2, 1, 0)]
-    state, near_rows = attend(
+    middle_places = [(2, 1, 0)]
+    far = [left2, left_across, right_across]
+    far_places = [(2, 0, 0), (3, 1, 0), (1, 1, 0)]
+    state, rows = attend(
         (0, 1), (qt, qt_twin), state_local, near, near_places, fresh=GROUPS
     )
-    near_twin = swapped(near_rows)
-    lent, far_rows = attend((1,), (qt_twin,), state, far, far_places, start=GROUPS)
+    state, rows = attend(
+        (0, 1), (qt, qt_twin), state, [opposite], middle_places, rows=(rows,)
+    )
+    lent, rows = attend(
+        (1,), (qt_twin,), state, far, far_places, start=GROUPS, rows=(rows,)
+    )
     sent = swapped(lent)
-    far_twin = swapped(far_rows)
+    twin_rows = swapped(rows)
     (mine,) = attend((0,), (qt,), state, far, far_places, pooled=0)
-    places = near_places + far_places
+    places = near_places + middle_places + far_places
     places = places + [(dx, dy, 1) for dx, dy, _ in places]
-    gap, grads = finish(
-        queries,
-        qt,
-        (state_local, mine, sent),
-        (near_rows, far_rows, near_twin, far_twin),
-        places,
-    )
+    gap, grads = finish(queries, qt, (state_local, mine, sent), (rows, twin_rows), places)
     arrived = lax.all_to_all(grads.reshape(SEQ, BEAC, 2 * HEAD), "seq", 0, 0, tiled=True)
     key_rows, value_rows = (
         jnp.sum(part.astype(F32), axis=0) for part in jnp.split(arrived, 2, axis=2)

time: 69.5 us -> 68.8 us (0.990)
  waiting for transfers between devices: 15.1 us -> 13 us
  Pallas kernels: 11 us -> 11.8 us
    ppermute x11 -> x10, waiting for transfers between devices: 15.1 us -> 13 us  [moved(): lax.ppermute(block, 'seq', [(s, placed(s, dx, dy, dc)) for s in range(SEQ)])]
    pallas_call x3 -> x4, Pallas kernels: 1.99 us -> 2.78 us  [attend(): pl.pallas_call(functools.partial(blocks_kernel, sides, start, fresh, pool...]
    ppermute x11 -> x10, starting transfers between devices: 16.4 us -> 16.4 us  [moved(): lax.ppermute(block, 'seq', [(s, placed(s, dx, dy, dc)) for s in range(SEQ)])]
  transfers between devices with their start and end apart: 11 -> 10, of which waited for: 8 -> 6; matrix products, arithmetic and copies ran while one was open for 0% -> 0% of each run, Pallas kernels for 4% -> 5%
where the time goes in v2:
time: 68.8 us; the launch traced here: 68.6 us
  blocking collectives  26.1 us (38%)
  starting transfers between devices  16.4 us (24%)
  waiting for transfers between devices  13 us (19%)
  Pallas kernels  11.8 us (17%)
  between operations  0.7 us (1%)
    all_to_all x1, blocking collectives, layer(): lax.all_to_all(grads.reshape(SEQ, BEAC, 2 * HEAD), 'seq', 0, 0, tiled=True)  26.1 us
    ppermute x10, starting transfers between devices, moved(): lax.ppermute(block, 'seq', [(s, placed(s, dx, dy, dc)) for s in range(SEQ)])  16.4 us
    ppermute x10, waiting for transfers between devices, moved(): lax.ppermute(block, 'seq', [(s, placed(s, dx, dy, dc)) for s in range(SEQ)])  13 us
    pallas_call x1, Pallas kernels, finish(): pl.pallas_call(functools.partial(final_kernel, counts, places), out_shape...  4.51 us
    pallas_call x1, Pallas kernels, local(): pl.pallas_call(local_kernel, out_shape=(QT_SHAPE, STATE), in_specs=[whole...  3.25 us
    pallas_call x4, Pallas kernels, attend(): pl.pallas_call(functools.partial(blocks_kernel, sides, start, fresh, pool...  2.78 us
  transfers between devices with their start and end apart: 10, of which 6 were waited for; matrix products, arithmetic and copies ran while one was open for 0% of the time, Pallas kernels for 5%

profile of v2, /device:TPU:1, one launch (start us, length us, event | category | flops | bytes accessed | tf_op | source)
XLA Modules:
  0.0 68.6 jit_solution(12023818138054969448)
XLA Ops:
  0.6 3.2 %local.1 = (bf16[2,128,1024]{2,1,0:T(8,128)(2,1)S(1)}, f32[2,144,1024]{2,1,0:T(8,128)S(1)}) custom-call(bf16[512,512]{1,0:T(8,128)(2,1)} %q_ref.1, bf16[512,128]{1,0:T(8,128)(2,1)} %keys_ref.3, bf16[512,128]{1,0:T(8,128)(2,1)} %values_ref.3), custom_call_target="tpu_custom_call" | custom-call | flops 536870912 | bytes 1048576 | tf_op jit(solution)/shard_map/local/pallas_call | solution.py:128
  3.9 3.3 %collective-permute-start = (bf16[2,128,1024]{2,1,0:T(8,128)(2,1)S(1)}, bf16[2,128,1024]{2,1,0:T(8,128)(2,1)S(1)}, u32[]{:S(2)}, u32[]{:S(2)}) collective-permute-start(bf16[2,128,1024]{2,1,0:T(8,128)(2,1)S(1)} %get-tuple-element.13.refs_0_.qt_ref), channel_id=1, source_target_pairs={{0,1},{1,0},{2,3},{3,2},{4,5},{5,4},{6,7},{7,6},{8,9},{9,8},{10,11... | collective-permute-start | bytes 1572872 | tf_op jit(solution)/shard_map/ppermute | solution.py:347
  7.2 1.2 %prep.1.refs_3_ = bf16[544,256]{1,0:T(8,128)(2,1)S(1)} custom-call(s32[32]{0:T(128)} %starts_ref.1, bf16[512,128]{1,0:T(8,128)(2,1)} %keys_ref.3, bf16[512,128]{1,0:T(8,128)(2,1)} %values_ref.3), custom_call_target="tpu_custom_call" | custom-call | tf_op jit(solution)/shard_map/prep/pallas_call | solution.py:57
  8.4 0.1 collective-permute-start.1
  8.5 2.4 %collective-permute-start.2 = (bf16[544,256]{1,0:T(8,128)(2,1)S(1)}, bf16[544,256]{1,0:T(8,128)(2,1)S(1)}, u32[]{:S(2)}, u32[]{:S(2)}) collective-permute-start(bf16[544,256]{1,0:T(8,128)(2,1)S(1)} %prep.1.refs_3_), channel_id=1, source_target_pairs={{0,2},{1,3},{2,0},{3,1},{4,6},{5,7},{6,4},{7,5},{8,10},{9,11},{10,... | collective-permute-start | bytes 835592 | tf_op jit(solution)/shard_map/ppermute | solution.py:347
  10.9 1.5 %collective-permute-start.3 = (bf16[544,256]{1,0:T(8,128)(2,1)S(1)}, bf16[544,256]{1,0:T(8,128)(2,1)S(1)}, u32[]{:S(2)}, u32[]{:S(2)}) collective-permute-start(bf16[544,256]{1,0:T(8,128)(2,1)S(1)} %prep.1.refs_3_), channel_id=1, source_target_pairs={{0,12},{1,13},{2,14},{3,15},{4,0},{5,1},{6,2},{7,3},{8,4},{9,5},{1... | collective-permute-start | bytes 835592 | tf_op jit(solution)/shard_map/ppermute | solution.py:347
  12.4 1.3 %collective-permute-start.4 = (bf16[544,256]{1,0:T(8,128)(2,1)S(1)}, bf16[544,256]{1,0:T(8,128)(2,1)S(1)}, u32[]{:S(2)}, u32[]{:S(2)}) collective-permute-start(bf16[544,256]{1,0:T(8,128)(2,1)S(1)} %prep.1.refs_3_), channel_id=1, source_target_pairs={{0,10},{1,11},{2,8},{3,9},{4,14},{5,15},{6,12},{7,13},{8,2},{9,3},... | collective-permute-start | bytes 835592 | tf_op jit(solution)/shard_map/ppermute | solution.py:347
  13.7 4.2 %collective-permute-done.1.refs_4_ = bf16[544,256]{1,0:T(8,128)(2,1)S(1)} collective-permute-done((bf16[544,256]{1,0:T(8,128)(2,1)S(1)}, bf16[544,256]{1,0:T(8,128)(2,1)S(1)}, u32[]{:S(2)}, u32[]{:S(2)}) %collective-permute-start.1) | collective-permute-done | bytes 278560 | tf_op jit(solution)/shard_map/ppermute | solution.py:347
  17.9 0.0 collective-permute-start.5
  17.9 0.4 collective-permute-done.2.refs_5_
  18.3 2.0 %collective-permute-start.6 = (bf16[544,256]{1,0:T(8,128)(2,1)S(1)}, bf16[544,256]{1,0:T(8,128)(2,1)S(1)}, u32[]{:S(2)}, u32[]{:S(2)}) collective-permute-start(bf16[544,256]{1,0:T(8,128)(2,1)S(1)} %collective-permute-done.1.refs_4_), channel_id=1, source_target_pairs={{0,2},{1,3},{2,0},{3,1},{4,6},{5,7},{6,4},{7,5},{8,10},{9,11},{10,... | collective-permute-start | bytes 835592 | tf_op jit(solution)/shard_map/ppermute | solution.py:347
  20.3 0.0 collective-permute-done.3.refs_6_
  20.3 1.5 %collective-permute-start.7 = (bf16[544,256]{1,0:T(8,128)(2,1)S(1)}, bf16[544,256]{1,0:T(8,128)(2,1)S(1)}, u32[]{:S(2)}, u32[]{:S(2)}) collective-permute-start(bf16[544,256]{1,0:T(8,128)(2,1)S(1)} %collective-permute-done.2.refs_5_), channel_id=1, source_target_pairs={{0,12},{1,13},{2,14},{3,15},{4,0},{5,1},{6,2},{7,3},{8,4},{9,5},{1... | collective-permute-start | bytes 835592 | tf_op jit(solution)/shard_map/ppermute | solution.py:347
  21.8 0.0 collective-permute-done.refs_1_.refs_0_
  21.8 0.7 %attend.4 = (f32[4,144,1024]{2,1,0:T(8,128)S(1)}, bf16[4,32,256]{2,1,0:T(8,128)(2,1)S(1)}) custom-call(bf16[2,128,1024]{2,1,0:T(8,128)(2,1)S(1)} %get-tuple-element.13.refs_0_.qt_ref, bf16[2,128,1024]{2,1,0:T(8,128)(2,1)S(1)} %collective-permute-done.refs_1_.refs_0_, f32[2,144,1024]{2,1,0:T(8,128)S(1)} %get-tuple-element.14.refs_2_.local_ref, ...), custom_call_target="tpu_custom_call" | custom-call | flops 4294967296 | bytes 1048576 | tf_op jit(solution)/shard_map/attend/pallas_call | solution.py:222
  22.5 3.3 %collective-permute-done.4.refs_3_ = bf16[544,256]{1,0:T(8,128)(2,1)S(1)} collective-permute-done((bf16[544,256]{1,0:T(8,128)(2,1)S(1)}, bf16[544,256]{1,0:T(8,128)(2,1)S(1)}, u32[]{:S(2)}, u32[]{:S(2)}) %collective-permute-start.4) | collective-permute-done | bytes 278560 | tf_op jit(solution)/shard_map/ppermute | solution.py:347
  25.8 0.7 attend.5
  26.5 0.5 collective-permute-done.5.refs_2_
  27.0 2.6 %collective-permute-done.6.refs_3_ = bf16[544,256]{1,0:T(8,128)(2,1)S(1)} collective-permute-done((bf16[544,256]{1,0:T(8,128)(2,1)S(1)}, bf16[544,256]{1,0:T(8,128)(2,1)S(1)}, u32[]{:S(2)}, u32[]{:S(2)}) %collective-permute-start.6) | collective-permute-done | bytes 278560 | tf_op jit(solution)/shard_map/ppermute | solution.py:347
  29.6 0.0 collective-permute-done.7.refs_4_
  29.6 0.8 %attend.7 = (f32[2,144,1024]{2,1,0:T(8,128)S(1)}, bf16[8,32,256]{2,1,0:T(8,128)(2,1)S(1)}) custom-call(bf16[2,128,1024]{2,1,0:T(8,128)(2,1)S(1)} %collective-permute-done.refs_1_.refs_0_, f32[4,144,1024]{2,1,0:T(8,128)S(1)} %get-tuple-element.17.refs_1_, bf16[544,256]{1,0:T(8,128)(2,1)S(1)} %collective-permute-done.5.refs_2_, ...), custom_call_target="tpu_custom_call" | custom-call | flops 1610612736 | bytes 1048576 | tf_op jit(solution)/shard_map/attend/pallas_call | solution.py:222
  30.4 4.2 %collective-permute-start.8 = (f32[2,144,1024]{2,1,0:T(8,128)S(1)}, f32[2,144,1024]{2,1,0:T(8,128)S(1)}, u32[]{:S(2)}, u32[]{:S(2)}) collective-permute-start(f32[2,144,1024]{2,1,0:T(8,128)S(1)} %get-tuple-element.19), channel_id=1, source_target_pairs={{0,1},{1,0},{2,3},{3,2},{4,5},{5,4},{6,7},{7,6},{8,9},{9,8},{10,11... | collective-permute-start | bytes 3538952 | tf_op jit(solution)/shard_map/ppermute | solution.py:347
  34.6 0.0 copy-start
  34.6 0.1 collective-permute-start.9
  34.7 0.6 attend.6.mine_ref
  35.3 1.9 %collective-permute-done.9.refs_1_ = bf16[8,32,256]{2,1,0:T(8,128)(2,1)S(1)} collective-permute-done((bf16[8,32,256]{2,1,0:T(8,128)(2,1)S(1)}, bf16[8,32,256]{2,1,0:T(8,128)(2,1)S(1)}, u32[]{:S(2)}, u32[]{:S(2)}) %collective-permute-start.9) | collective-permute-done | bytes 131104 | tf_op jit(solution)/shard_map/ppermute | solution.py:347
  37.3 0.0 collective-permute-done.8.sent_ref
  37.3 0.0 copy-done
  37.3 4.5 %finish.1 = (bf16[512,512]{1,0:T(8,128)(2,1)}, bf16[512,256]{1,0:T(8,128)(2,1)S(1)}) custom-call(bf16[512,512]{1,0:T(8,128)(2,1)S(1)} %copy-done, bf16[2,128,1024]{2,1,0:T(8,128)(2,1)S(1)} %get-tuple-element.13.refs_0_.qt_ref, f32[2,144,1024]{2,1,0:T(8,128)S(1)} %get-tuple-element.14.refs_2_.local_ref, f32[2,144,1024]{2,1,0:T(8,128)S(1)} %attend.6.mine_ref, ...), custom_call_target="tpu_custom_call" | custom-call | flops 1073741824 | bytes 1048576 | tf_op jit(solution)/shard_map/finish/pallas_call | solution.py:316
  41.8 26.1 %all_to_all.5 = bf16[16,32,256]{2,1,0:T(8,128)(2,1)S(1)} all-to-all(bf16[16,32,256]{2,1,0:T(8,128)(2,1)S(1)} %bitcast.1), channel_id=1, replica_groups=mesh['doc'=16,'seq'=16] {'seq'}, dimensions={0} | all-to-all | bytes 524288 | tf_op jit(solution)/shard_map/all_to_all | solution.py:385
  68.0 0.6 convert_reduce_fusion
Async XLA Ops:
  3.9 17.9 %collective-permute-start = (bf16[2,128,1024]{2,1,0:T(8,128)(2,1)S(1)}, bf16[2,128,1024]{2,1,0:T(8,128)(2,1)S(1)}, u32[]{:S(2)}, u32[]{:S(2)}) collective-permute-start(bf16[2,128,1024]{2,1,0:T(8,128)(2,1)S(1)} %get-tuple-element.13.refs_0_.qt_ref), channel_id=1, source_target_pairs={{0,1},{1,0},{2,3},{3,2},{4,5},{5,4},{6,7},{7,6},{8,9},{9,8},{10,11... | collective-permute-start | bytes 1572872 | tf_op jit(solution)/shard_map/ppermute | solution.py:347
  8.4 9.5 %collective-permute-start.1 = (bf16[544,256]{1,0:T(8,128)(2,1)S(1)}, bf16[544,256]{1,0:T(8,128)(2,1)S(1)}, u32[]{:S(2)}, u32[]{:S(2)}) collective-permute-start(bf16[544,256]{1,0:T(8,128)(2,1)S(1)} %prep.1.refs_3_), channel_id=1, source_target_pairs={{0,4},{1,5},{2,6},{3,7},{4,8},{5,9},{6,10},{7,11},{8,12},{9,13},{1... | collective-permute-start | bytes 835592 | tf_op jit(solution)/shard_map/ppermute | solution.py:347
  8.5 9.8 %collective-permute-start.2 = (bf16[544,256]{1,0:T(8,128)(2,1)S(1)}, bf16[544,256]{1,0:T(8,128)(2,1)S(1)}, u32[]{:S(2)}, u32[]{:S(2)}) collective-permute-start(bf16[544,256]{1,0:T(8,128)(2,1)S(1)} %prep.1.refs_3_), channel_id=1, source_target_pairs={{0,2},{1,3},{2,0},{3,1},{4,6},{5,7},{6,4},{7,5},{8,10},{9,11},{10,... | collective-permute-start | bytes 835592 | tf_op jit(solution)/shard_map/ppermute | solution.py:347
  10.9 9.4 %collective-permute-start.3 = (bf16[544,256]{1,0:T(8,128)(2,1)S(1)}, bf16[544,256]{1,0:T(8,128)(2,1)S(1)}, u32[]{:S(2)}, u32[]{:S(2)}) collective-permute-start(bf16[544,256]{1,0:T(8,128)(2,1)S(1)} %prep.1.refs_3_), channel_id=1, source_target_pairs={{0,12},{1,13},{2,14},{3,15},{4,0},{5,1},{6,2},{7,3},{8,4},{9,5},{1... | collective-permute-start | bytes 835592 | tf_op jit(solution)/shard_map/ppermute | solution.py:347
  12.4 13.4 %collective-permute-start.4 = (bf16[544,256]{1,0:T(8,128)(2,1)S(1)}, bf16[544,256]{1,0:T(8,128)(2,1)S(1)}, u32[]{:S(2)}, u32[]{:S(2)}) collective-permute-start(bf16[544,256]{1,0:T(8,128)(2,1)S(1)} %prep.1.refs_3_), channel_id=1, source_target_pairs={{0,10},{1,11},{2,8},{3,9},{4,14},{5,15},{6,12},{7,13},{8,2},{9,3},... | collective-permute-start | bytes 835592 | tf_op jit(solution)/shard_map/ppermute | solution.py:347
  17.9 9.1 %collective-permute-start.5 = (bf16[544,256]{1,0:T(8,128)(2,1)S(1)}, bf16[544,256]{1,0:T(8,128)(2,1)S(1)}, u32[]{:S(2)}, u32[]{:S(2)}) collective-permute-start(bf16[544,256]{1,0:T(8,128)(2,1)S(1)} %collective-permute-done.1.refs_4_), channel_id=1, source_target_pairs={{0,4},{1,5},{2,6},{3,7},{4,8},{5,9},{6,10},{7,11},{8,12},{9,13},{1... | collective-permute-start | bytes 835592 | tf_op jit(solution)/shard_map/ppermute | solution.py:347
  18.3 11.4 %collective-permute-start.6 = (bf16[544,256]{1,0:T(8,128)(2,1)S(1)}, bf16[544,256]{1,0:T(8,128)(2,1)S(1)}, u32[]{:S(2)}, u32[]{:S(2)}) collective-permute-start(bf16[544,256]{1,0:T(8,128)(2,1)S(1)} %collective-permute-done.1.refs_4_), channel_id=1, source_target_pairs={{0,2},{1,3},{2,0},{3,1},{4,6},{5,7},{6,4},{7,5},{8,10},{9,11},{10,... | collective-permute-start | bytes 835592 | tf_op jit(solution)/shard_map/ppermute | solution.py:347
  20.3 9.3 %collective-permute-start.7 = (bf16[544,256]{1,0:T(8,128)(2,1)S(1)}, bf16[544,256]{1,0:T(8,128)(2,1)S(1)}, u32[]{:S(2)}, u32[]{:S(2)}) collective-permute-start(bf16[544,256]{1,0:T(8,128)(2,1)S(1)} %collective-permute-done.2.refs_5_), channel_id=1, source_target_pairs={{0,12},{1,13},{2,14},{3,15},{4,0},{5,1},{6,2},{7,3},{8,4},{9,5},{1... | collective-permute-start | bytes 835592 | tf_op jit(solution)/shard_map/ppermute | solution.py:347
  30.4 6.9 %collective-permute-start.8 = (f32[2,144,1024]{2,1,0:T(8,128)S(1)}, f32[2,144,1024]{2,1,0:T(8,128)S(1)}, u32[]{:S(2)}, u32[]{:S(2)}) collective-permute-start(f32[2,144,1024]{2,1,0:T(8,128)S(1)} %get-tuple-element.19), channel_id=1, source_target_pairs={{0,1},{1,0},{2,3},{3,2},{4,5},{5,4},{6,7},{7,6},{8,9},{9,8},{10,11... | collective-permute-start | bytes 3538952 | tf_op jit(solution)/shard_map/ppermute | solution.py:347
  34.6 2.7 %copy-start = (bf16[512,512]{1,0:T(8,128)(2,1)S(1)}, bf16[512,512]{1,0:T(8,128)(2,1)}, u32[]{:S(2)}) copy-start(bf16[512,512]{1,0:T(8,128)(2,1)} %q_ref.1) | copy-start | bytes 1572868
  34.6 2.7 %collective-permute-start.9 = (bf16[8,32,256]{2,1,0:T(8,128)(2,1)S(1)}, bf16[8,32,256]{2,1,0:T(8,128)(2,1)S(1)}, u32[]{:S(2)}, u32[]{:S(2)}) collective-permute-start(bf16[8,32,256]{2,1,0:T(8,128)(2,1)S(1)} %get-tuple-element.20.refs_0_), channel_id=1, source_target_pairs={{0,1},{1,0},{2,3},{3,2},{4,5},{5,4},{6,7},{7,6},{8,9},{9,8},{10,11... | collective-permute-start | bytes 393224 | tf_op jit(solution)/shard_map/ppermute | solution.py:347

commit v3 on v2

--- a/solution.py
+++ b/solution.py
@@ -192,7 +192,7 @@
     def step(t, carry):
         gather(t - 1)
         weigh(t)
-        score(jnp.minimum(t + 1, tiles - 1))
+        score(t + 1)
         return carry
 
     score(0)
@@ -208,7 +208,9 @@
     def _():
         weigh(0)
         score(1)
-        lax.fori_loop(1, tiles, step, 0)
+        lax.fori_loop(1, tiles - 1, step, 0)
+        gather(tiles - 2)
+        weigh(tiles - 1)
         gather(tiles - 1)
 
     for g in range(groups):

time: 68.8 us -> 67.6 us (0.983)
  blocking collectives: 26.1 us -> 25.1 us
    all_to_all x1, blocking collectives: 26.1 us -> 25.1 us  [layer(): lax.all_to_all(grads.reshape(SEQ, BEAC, 2 * HEAD), 'seq', 0, 0, tiled=True)]
where the time goes in v3:
time: 67.6 us; the launch traced here: 67.4 us
  blocking collectives  25.1 us (37%)
  starting transfers between devices  16.4 us (24%)
  waiting for transfers between devices  12.8 us (19%)
  Pallas kernels  11.8 us (17%)
  between operations  0.7 us (1%)
    all_to_all x1, blocking collectives, layer(): lax.all_to_all(grads.reshape(SEQ, BEAC, 2 * HEAD), 'seq', 0, 0, tiled=True)  25.1 us
    ppermute x10, starting transfers between devices, moved(): lax.ppermute(block, 'seq', [(s, placed(s, dx, dy, dc)) for s in range(SEQ)])  16.4 us
    ppermute x10, waiting for transfers between devices, moved(): lax.ppermute(block, 'seq', [(s, placed(s, dx, dy, dc)) for s in range(SEQ)])  12.8 us
    pallas_call x1, Pallas kernels, finish(): pl.pallas_call(functools.partial(final_kernel, counts, places), out_shape...  4.53 us
    pallas_call x1, Pallas kernels, local(): pl.pallas_call(local_kernel, out_shape=(QT_SHAPE, STATE), in_specs=[whole...  3.25 us
    pallas_call x4, Pallas kernels, attend(): pl.pallas_call(functools.partial(blocks_kernel, sides, start, fresh, pool...  2.78 us
  transfers between devices with their start and end apart: 10, of which 6 were waited for; matrix products, arithmetic and copies ran while one was open for 0% of the time, Pallas kernels for 5%

profile of v3, /device:TPU:1, one launch (start us, length us, event | category | flops | bytes accessed | tf_op | source)
XLA Modules:
  0.0 67.4 jit_solution(10565786018625170622)
XLA Ops:
  0.6 3.2 %local.1 = (bf16[2,128,1024]{2,1,0:T(8,128)(2,1)S(1)}, f32[2,144,1024]{2,1,0:T(8,128)S(1)}) custom-call(bf16[512,512]{1,0:T(8,128)(2,1)} %q_ref.1, bf16[512,128]{1,0:T(8,128)(2,1)} %keys_ref.3, bf16[512,128]{1,0:T(8,128)(2,1)} %values_ref.3), custom_call_target="tpu_custom_call" | custom-call | flops 536870912 | bytes 1048576 | tf_op jit(solution)/shard_map/local/pallas_call | solution.py:128
  3.9 3.3 %collective-permute-start = (bf16[2,128,1024]{2,1,0:T(8,128)(2,1)S(1)}, bf16[2,128,1024]{2,1,0:T(8,128)(2,1)S(1)}, u32[]{:S(2)}, u32[]{:S(2)}) collective-permute-start(bf16[2,128,1024]{2,1,0:T(8,128)(2,1)S(1)} %get-tuple-element.13.refs_0_.qt_ref), channel_id=1, source_target_pairs={{0,1},{1,0},{2,3},{3,2},{4,5},{5,4},{6,7},{7,6},{8,9},{9,8},{10,11... | collective-permute-start | bytes 1572872 | tf_op jit(solution)/shard_map/ppermute | solution.py:349
  7.2 1.2 %prep.1.refs_3_ = bf16[544,256]{1,0:T(8,128)(2,1)S(1)} custom-call(s32[32]{0:T(128)} %starts_ref.1, bf16[512,128]{1,0:T(8,128)(2,1)} %keys_ref.3, bf16[512,128]{1,0:T(8,128)(2,1)} %values_ref.3), custom_call_target="tpu_custom_call" | custom-call | tf_op jit(solution)/shard_map/prep/pallas_call | solution.py:57
  8.4 0.1 collective-permute-start.1
  8.5 2.4 %collective-permute-start.2 = (bf16[544,256]{1,0:T(8,128)(2,1)S(1)}, bf16[544,256]{1,0:T(8,128)(2,1)S(1)}, u32[]{:S(2)}, u32[]{:S(2)}) collective-permute-start(bf16[544,256]{1,0:T(8,128)(2,1)S(1)} %prep.1.refs_3_), channel_id=1, source_target_pairs={{0,2},{1,3},{2,0},{3,1},{4,6},{5,7},{6,4},{7,5},{8,10},{9,11},{10,... | collective-permute-start | bytes 835592 | tf_op jit(solution)/shard_map/ppermute | solution.py:349
  10.9 1.5 %collective-permute-start.3 = (bf16[544,256]{1,0:T(8,128)(2,1)S(1)}, bf16[544,256]{1,0:T(8,128)(2,1)S(1)}, u32[]{:S(2)}, u32[]{:S(2)}) collective-permute-start(bf16[544,256]{1,0:T(8,128)(2,1)S(1)} %prep.1.refs_3_), channel_id=1, source_target_pairs={{0,12},{1,13},{2,14},{3,15},{4,0},{5,1},{6,2},{7,3},{8,4},{9,5},{1... | collective-permute-start | bytes 835592 | tf_op jit(solution)/shard_map/ppermute | solution.py:349
  12.4 1.3 %collective-permute-start.4 = (bf16[544,256]{1,0:T(8,128)(2,1)S(1)}, bf16[544,256]{1,0:T(8,128)(2,1)S(1)}, u32[]{:S(2)}, u32[]{:S(2)}) collective-permute-start(bf16[544,256]{1,0:T(8,128)(2,1)S(1)} %prep.1.refs_3_), channel_id=1, source_target_pairs={{0,10},{1,11},{2,8},{3,9},{4,14},{5,15},{6,12},{7,13},{8,2},{9,3},... | collective-permute-start | bytes 835592 | tf_op jit(solution)/shard_map/ppermute | solution.py:349
  13.7 4.2 %collective-permute-done.1.refs_4_ = bf16[544,256]{1,0:T(8,128)(2,1)S(1)} collective-permute-done((bf16[544,256]{1,0:T(8,128)(2,1)S(1)}, bf16[544,256]{1,0:T(8,128)(2,1)S(1)}, u32[]{:S(2)}, u32[]{:S(2)}) %collective-permute-start.1) | collective-permute-done | bytes 278560 | tf_op jit(solution)/shard_map/ppermute | solution.py:349
  17.9 0.0 collective-permute-start.5
  17.9 0.4 collective-permute-done.2.refs_5_
  18.3 2.0 %collective-permute-start.6 = (bf16[544,256]{1,0:T(8,128)(2,1)S(1)}, bf16[544,256]{1,0:T(8,128)(2,1)S(1)}, u32[]{:S(2)}, u32[]{:S(2)}) collective-permute-start(bf16[544,256]{1,0:T(8,128)(2,1)S(1)} %collective-permute-done.1.refs_4_), channel_id=1, source_target_pairs={{0,2},{1,3},{2,0},{3,1},{4,6},{5,7},{6,4},{7,5},{8,10},{9,11},{10,... | collective-permute-start | bytes 835592 | tf_op jit(solution)/shard_map/ppermute | solution.py:349
  20.3 0.0 collective-permute-done.3.refs_6_
  20.3 1.5 %collective-permute-start.7 = (bf16[544,256]{1,0:T(8,128)(2,1)S(1)}, bf16[544,256]{1,0:T(8,128)(2,1)S(1)}, u32[]{:S(2)}, u32[]{:S(2)}) collective-permute-start(bf16[544,256]{1,0:T(8,128)(2,1)S(1)} %collective-permute-done.2.refs_5_), channel_id=1, source_target_pairs={{0,12},{1,13},{2,14},{3,15},{4,0},{5,1},{6,2},{7,3},{8,4},{9,5},{1... | collective-permute-start | bytes 835592 | tf_op jit(solution)/shard_map/ppermute | solution.py:349
  21.8 0.0 collective-permute-done.refs_1_.refs_0_
  21.8 0.7 %attend.4 = (f32[4,144,1024]{2,1,0:T(8,128)S(1)}, bf16[4,32,256]{2,1,0:T(8,128)(2,1)S(1)}) custom-call(bf16[2,128,1024]{2,1,0:T(8,128)(2,1)S(1)} %get-tuple-element.13.refs_0_.qt_ref, bf16[2,128,1024]{2,1,0:T(8,128)(2,1)S(1)} %collective-permute-done.refs_1_.refs_0_, f32[2,144,1024]{2,1,0:T(8,128)S(1)} %get-tuple-element.14.refs_2_.local_ref, ...), custom_call_target="tpu_custom_call" | custom-call | flops 4294967296 | bytes 1048576 | tf_op jit(solution)/shard_map/attend/pallas_call | solution.py:224
  22.5 3.3 %collective-permute-done.4.refs_3_ = bf16[544,256]{1,0:T(8,128)(2,1)S(1)} collective-permute-done((bf16[544,256]{1,0:T(8,128)(2,1)S(1)}, bf16[544,256]{1,0:T(8,128)(2,1)S(1)}, u32[]{:S(2)}, u32[]{:S(2)}) %collective-permute-start.4) | collective-permute-done | bytes 278560 | tf_op jit(solution)/shard_map/ppermute | solution.py:349
  25.8 0.9 %attend.5 = (f32[4,144,1024]{2,1,0:T(8,128)S(1)}, bf16[5,32,256]{2,1,0:T(8,128)(2,1)S(1)}) custom-call(bf16[2,128,1024]{2,1,0:T(8,128)(2,1)S(1)} %get-tuple-element.13.refs_0_.qt_ref, bf16[2,128,1024]{2,1,0:T(8,128)(2,1)S(1)} %collective-permute-done.refs_1_.refs_0_, f32[4,144,1024]{2,1,0:T(8,128)S(1)} %get-tuple-element.15.refs_2_, ...), custom_call_target="tpu_custom_call" | custom-call | flops 1073741824 | bytes 1048576 | tf_op jit(solution)/shard_map/attend/pallas_call | solution.py:224
  26.7 0.4 collective-permute-done.5.refs_2_
  27.0 2.6 %collective-permute-done.6.refs_3_ = bf16[544,256]{1,0:T(8,128)(2,1)S(1)} collective-permute-done((bf16[544,256]{1,0:T(8,128)(2,1)S(1)}, bf16[544,256]{1,0:T(8,128)(2,1)S(1)}, u32[]{:S(2)}, u32[]{:S(2)}) %collective-permute-start.6) | collective-permute-done | bytes 278560 | tf_op jit(solution)/shard_map/ppermute | solution.py:349
  29.6 0.0 collective-permute-done.7.refs_4_
  29.6 0.6 attend.7
  30.2 4.2 %collective-permute-start.8 = (f32[2,144,1024]{2,1,0:T(8,128)S(1)}, f32[2,144,1024]{2,1,0:T(8,128)S(1)}, u32[]{:S(2)}, u32[]{:S(2)}) collective-permute-start(f32[2,144,1024]{2,1,0:T(8,128)S(1)} %get-tuple-element.19), channel_id=1, source_target_pairs={{0,1},{1,0},{2,3},{3,2},{4,5},{5,4},{6,7},{7,6},{8,9},{9,8},{10,11... | collective-permute-start | bytes 3538952 | tf_op jit(solution)/shard_map/ppermute | solution.py:349
  34.4 0.0 copy-start
  34.4 0.1 collective-permute-start.9
  34.6 0.6 attend.6.mine_ref
  35.2 1.9 %collective-permute-done.9.refs_1_ = bf16[8,32,256]{2,1,0:T(8,128)(2,1)S(1)} collective-permute-done((bf16[8,32,256]{2,1,0:T(8,128)(2,1)S(1)}, bf16[8,32,256]{2,1,0:T(8,128)(2,1)S(1)}, u32[]{:S(2)}, u32[]{:S(2)}) %collective-permute-start.9) | collective-permute-done | bytes 131104 | tf_op jit(solution)/shard_map/ppermute | solution.py:349
  37.1 0.0 collective-permute-done.8.sent_ref
  37.1 0.0 copy-done
  37.1 4.5 %finish.1 = (bf16[512,512]{1,0:T(8,128)(2,1)}, bf16[512,256]{1,0:T(8,128)(2,1)S(1)}) custom-call(bf16[512,512]{1,0:T(8,128)(2,1)S(1)} %copy-done, bf16[2,128,1024]{2,1,0:T(8,128)(2,1)S(1)} %get-tuple-element.13.refs_0_.qt_ref, f32[2,144,1024]{2,1,0:T(8,128)S(1)} %get-tuple-element.14.refs_2_.local_ref, f32[2,144,1024]{2,1,0:T(8,128)S(1)} %attend.6.mine_ref, ...), custom_call_target="tpu_custom_call" | custom-call | flops 1073741824 | bytes 1048576 | tf_op jit(solution)/shard_map/finish/pallas_call | solution.py:318
  41.6 25.1 %all_to_all.5 = bf16[16,32,256]{2,1,0:T(8,128)(2,1)S(1)} all-to-all(bf16[16,32,256]{2,1,0:T(8,128)(2,1)S(1)} %bitcast.1), channel_id=1, replica_groups=mesh['doc'=16,'seq'=16] {'seq'}, dimensions={0} | all-to-all | bytes 524288 | tf_op jit(solution)/shard_map/all_to_all | solution.py:387
  66.8 0.6 convert_reduce_fusion
Async XLA Ops:
  3.9 17.9 %collective-permute-start = (bf16[2,128,1024]{2,1,0:T(8,128)(2,1)S(1)}, bf16[2,128,1024]{2,1,0:T(8,128)(2,1)S(1)}, u32[]{:S(2)}, u32[]{:S(2)}) collective-permute-start(bf16[2,128,1024]{2,1,0:T(8,128)(2,1)S(1)} %get-tuple-element.13.refs_0_.qt_ref), channel_id=1, source_target_pairs={{0,1},{1,0},{2,3},{3,2},{4,5},{5,4},{6,7},{7,6},{8,9},{9,8},{10,11... | collective-permute-start | bytes 1572872 | tf_op jit(solution)/shard_map/ppermute | solution.py:349
  8.4 9.5 %collective-permute-start.1 = (bf16[544,256]{1,0:T(8,128)(2,1)S(1)}, bf16[544,256]{1,0:T(8,128)(2,1)S(1)}, u32[]{:S(2)}, u32[]{:S(2)}) collective-permute-start(bf16[544,256]{1,0:T(8,128)(2,1)S(1)} %prep.1.refs_3_), channel_id=1, source_target_pairs={{0,4},{1,5},{2,6},{3,7},{4,8},{5,9},{6,10},{7,11},{8,12},{9,13},{1... | collective-permute-start | bytes 835592 | tf_op jit(solution)/shard_map/ppermute | solution.py:349
  8.5 9.8 %collective-permute-start.2 = (bf16[544,256]{1,0:T(8,128)(2,1)S(1)}, bf16[544,256]{1,0:T(8,128)(2,1)S(1)}, u32[]{:S(2)}, u32[]{:S(2)}) collective-permute-start(bf16[544,256]{1,0:T(8,128)(2,1)S(1)} %prep.1.refs_3_), channel_id=1, source_target_pairs={{0,2},{1,3},{2,0},{3,1},{4,6},{5,7},{6,4},{7,5},{8,10},{9,11},{10,... | collective-permute-start | bytes 835592 | tf_op jit(solution)/shard_map/ppermute | solution.py:349
  10.9 9.4 %collective-permute-start.3 = (bf16[544,256]{1,0:T(8,128)(2,1)S(1)}, bf16[544,256]{1,0:T(8,128)(2,1)S(1)}, u32[]{:S(2)}, u32[]{:S(2)}) collective-permute-start(bf16[544,256]{1,0:T(8,128)(2,1)S(1)} %prep.1.refs_3_), channel_id=1, source_target_pairs={{0,12},{1,13},{2,14},{3,15},{4,0},{5,1},{6,2},{7,3},{8,4},{9,5},{1... | collective-permute-start | bytes 835592 | tf_op jit(solution)/shard_map/ppermute | solution.py:349
  12.4 13.4 %collective-permute-start.4 = (bf16[544,256]{1,0:T(8,128)(2,1)S(1)}, bf16[544,256]{1,0:T(8,128)(2,1)S(1)}, u32[]{:S(2)}, u32[]{:S(2)}) collective-permute-start(bf16[544,256]{1,0:T(8,128)(2,1)S(1)} %prep.1.refs_3_), channel_id=1, source_target_pairs={{0,10},{1,11},{2,8},{3,9},{4,14},{5,15},{6,12},{7,13},{8,2},{9,3},... | collective-permute-start | bytes 835592 | tf_op jit(solution)/shard_map/ppermute | solution.py:349
  17.9 9.1 %collective-permute-start.5 = (bf16[544,256]{1,0:T(8,128)(2,1)S(1)}, bf16[544,256]{1,0:T(8,128)(2,1)S(1)}, u32[]{:S(2)}, u32[]{:S(2)}) collective-permute-start(bf16[544,256]{1,0:T(8,128)(2,1)S(1)} %collective-permute-done.1.refs_4_), channel_id=1, source_target_pairs={{0,4},{1,5},{2,6},{3,7},{4,8},{5,9},{6,10},{7,11},{8,12},{9,13},{1... | collective-permute-start | bytes 835592 | tf_op jit(solution)/shard_map/ppermute | solution.py:349
  18.3 11.4 %collective-permute-start.6 = (bf16[544,256]{1,0:T(8,128)(2,1)S(1)}, bf16[544,256]{1,0:T(8,128)(2,1)S(1)}, u32[]{:S(2)}, u32[]{:S(2)}) collective-permute-start(bf16[544,256]{1,0:T(8,128)(2,1)S(1)} %collective-permute-done.1.refs_4_), channel_id=1, source_target_pairs={{0,2},{1,3},{2,0},{3,1},{4,6},{5,7},{6,4},{7,5},{8,10},{9,11},{10,... | collective-permute-start | bytes 835592 | tf_op jit(solution)/shard_map/ppermute | solution.py:349
  20.3 9.3 %collective-permute-start.7 = (bf16[544,256]{1,0:T(8,128)(2,1)S(1)}, bf16[544,256]{1,0:T(8,128)(2,1)S(1)}, u32[]{:S(2)}, u32[]{:S(2)}) collective-permute-start(bf16[544,256]{1,0:T(8,128)(2,1)S(1)} %collective-permute-done.2.refs_5_), channel_id=1, source_target_pairs={{0,12},{1,13},{2,14},{3,15},{4,0},{5,1},{6,2},{7,3},{8,4},{9,5},{1... | collective-permute-start | bytes 835592 | tf_op jit(solution)/shard_map/ppermute | solution.py:349
  30.2 6.9 %collective-permute-start.8 = (f32[2,144,1024]{2,1,0:T(8,128)S(1)}, f32[2,144,1024]{2,1,0:T(8,128)S(1)}, u32[]{:S(2)}, u32[]{:S(2)}) collective-permute-start(f32[2,144,1024]{2,1,0:T(8,128)S(1)} %get-tuple-element.19), channel_id=1, source_target_pairs={{0,1},{1,0},{2,3},{3,2},{4,5},{5,4},{6,7},{7,6},{8,9},{9,8},{10,11... | collective-permute-start | bytes 3538952 | tf_op jit(solution)/shard_map/ppermute | solution.py:349
  34.4 2.7 %copy-start = (bf16[512,512]{1,0:T(8,128)(2,1)S(1)}, bf16[512,512]{1,0:T(8,128)(2,1)}, u32[]{:S(2)}) copy-start(bf16[512,512]{1,0:T(8,128)(2,1)} %q_ref.1) | copy-start | bytes 1572868
  34.4 2.7 %collective-permute-start.9 = (bf16[8,32,256]{2,1,0:T(8,128)(2,1)S(1)}, bf16[8,32,256]{2,1,0:T(8,128)(2,1)S(1)}, u32[]{:S(2)}, u32[]{:S(2)}) collective-permute-start(bf16[8,32,256]{2,1,0:T(8,128)(2,1)S(1)} %get-tuple-element.20.refs_0_), channel_id=1, source_target_pairs={{0,1},{1,0},{2,3},{3,2},{4,5},{5,4},{6,7},{7,6},{8,9},{9,8},{10,11... | collective-permute-start | bytes 393224 | tf_op jit(solution)/shard_map/ppermute | solution.py:349
